TPU v7x, 32 devices: a whole 2x2x4 slice. The times are simulated.
32 devices in a mesh: role: 2 (over x), gy: 2 (over y), gx: 8 (over z, core).
Axes of the slice: x: 2, y: 2, z: 4, core: 2. Of those that a mesh axis runs over, the one named last changes fastest.
Arguments:
- thermal_anomaly: float32 [16, 192, 2048], P('role', 'gy', 'gx'), may hold values from -6 to 6
- saltiness_anomaly: float32 [16, 192, 2048], P('role', 'gy', 'gx'), may hold values from -6 to 6
- zonal_flow_fraction: bfloat16 [16, 192, 2048], P('role', 'gy', 'gx'), may hold values from -0.5 to 0.5
- meridional_flow_fraction: bfloat16 [16, 192, 2048], P('role', 'gy', 'gx'), may hold values from -0.5 to 0.5
- mixing_coefficient: float32 [16], P('role'), may hold values from 0.03 to 0.2
- continent_patch_numbering: int32 [2], replicated, may hold values from 0 to 15
- parallel_band_coefficients: bfloat16 [16, 4, 12], P('gy'), may hold values from -1.75 to 1.75
- meridian_panel_coefficients: bfloat16 [14, 512, 128], replicated, may hold values from -0.25 to 0.25
- panel_starting_source_meridian: int32 [14], replicated, may hold values from 0 to 1536, as said below
- target_parallel_cluster: int32 [64], replicated, may hold values from 0 to 7, as said below
Outputs:
- remapped: bfloat16 [3, 16, 64, 1792], P(None, 'role', ('gy', 'gx'))
- checksums: float32 [3, 8], replicated
Inputs may be any that keep to these rules, and one draw needn't show every extreme that they name: `panel_starting_source_meridian`: every block's window lies within the model grid. `target_parallel_cluster`: each group number names exactly 8 rows.
All inputs are finite; a program needn't handle non-finite values.
Results may differ from a plain program's by a relative error of at most 0.0057.
Values may be sent and summed in bfloat16 or wider, within the bound.
A program may use at most 64 MiB of HBM per device.

v0:
```python
import functools
import math

import jax
import jax.numpy as jnp
import numpy as np
from jax import lax
from jax.experimental import pallas as pl
from jax.experimental.pallas import tpu as pltpu
from jax.sharding import PartitionSpec as P

LANES = 128
F32 = jnp.float32
BF16 = jnp.bfloat16
MESH = pl.DeviceIdType.MESH


def wrap(value, count):
    return jnp.where(value >= count, value - count, value)


def iota(shape, dim):
    return lax.broadcasted_iota(jnp.int32, shape, dim)


def peer_of(dims, d):
    n_role, n_gy, n_gx = dims[:3]
    role, gy, gx = (lax.axis_index(a) for a in ("role", "gy", "gx"))
    dx, dyr = d % n_gx, d // n_gx
    dy, dr = dyr % n_gy, dyr // n_gy
    return (wrap(role + dr, n_role), wrap(gy + dy, n_gy), wrap(gx + dx, n_gx))


def model_kernel(
    dims,
    temp_hbm,
    salt_hbm,
    zonal_hbm,
    merid_hbm,
    kappa_ref,
    land_ref,
    band_ref,
    lat_out,
    x0,
    x1,
    zonal,
    merid,
    band_rows,
    means,
    lat_send,
    lat_recv,
    row_send,
    row_recv,
    col_send,
    col_recv,
    in_sems,
    halo_send_sems,
    halo_recv_sems,
    a2a_send_sems,
    a2a_recv_sems,
    local_sems,
    out_sems,
):
    n_role, n_gy, n_gx, levels, cy, cx, trows, srows, nblk, sw, tb, groups = dims
    role, gy, gx = (lax.axis_index(a) for a in ("role", "gy", "gx"))
    lev_grp = 16 // trows
    halves = levels // lev_grp

    loads = [
        pltpu.make_async_copy(temp_hbm, x0.at[0], in_sems.at[0]),
        pltpu.make_async_copy(salt_hbm, x0.at[1], in_sems.at[1]),
        pltpu.make_async_copy(zonal_hbm, zonal, in_sems.at[2]),
        pltpu.make_async_copy(merid_hbm, merid, in_sems.at[3]),
    ]
    for load in loads:
        load.start()

    peer = functools.partial(peer_of, dims)
    barrier = pltpu.get_barrier_semaphore()
    greeted = [d for d in range(1, n_gx)] + [d * n_gx for d in range(1, n_role * n_gy)]
    for d in greeted:
        pl.semaphore_signal(barrier, inc=1, device_id=peer(d), device_id_type=MESH)

    band_rows[...] = jnp.zeros_like(band_rows)

    lane = iota((cy, LANES), 1)

    def pack_columns(s, tiles):
        first = jnp.zeros((cy, LANES), F32)
        last = jnp.zeros((cy, LANES), F32)
        for t in range(2):
            for l in range(levels):
                k = t * levels + l
                head = tiles[t, l, :, pl.ds(0, LANES)]
                tail = tiles[t, l, :, pl.ds(cx - LANES, LANES)]
                first = jnp.where(lane == k, pltpu.roll(head, k, 1) if k else head, first)
                last = jnp.where(lane == k, pltpu.roll(tail, k + 1, 1), last)
        col_send[s, 0] = first
        col_send[s, 1] = last

    def pack_rows(s, t, l, head, tail):
        row_send[s, 0, t, pl.ds(l, 1), :] = head
        row_send[s, 1, t, pl.ds(l, 1), :] = tail

    west = wrap(gx + n_gx - 1, n_gx)
    east = wrap(gx + 1, n_gx)
    below = wrap(gy + n_gy - 1, n_gy)
    above = wrap(gy + 1, n_gy)

    def halo_copies(s):
        copies = []
        for i, (send, recv, d, target) in enumerate(
            (
                (col_send, col_recv, 0, (role, gy, west)),
                (col_send, col_recv, 1, (role, gy, east)),
                (row_send, row_recv, 0, (role, below, gx)),
                (row_send, row_recv, 1, (role, above, gx)),
            )
        ):
            copies.append(
                pltpu.make_async_remote_copy(
                    src_ref=send.at[s, d],
                    dst_ref=recv.at[s, d],
                    send_sem=halo_send_sems.at[s, i],
                    recv_sem=halo_recv_sems.at[s, i],
                    device_id=target,
                    device_id_type=MESH,
                )
            )
        return copies

    loads[0].wait()
    loads[1].wait()
    for t in range(2):
        for l in range(levels):
            pack_rows(0, t, l, x0[t, l, pl.ds(0, 1), :], x0[t, l, pl.ds(cy - 1, 1), :])
    pack_columns(0, x0)
    pl.semaphore_wait(barrier, len(greeted))
    halo0 = halo_copies(0)
    for copy in halo0:
        copy.start()

    for g in range(n_gx):
        band_rows[pl.ds(g * trows, trows), pl.ds(0, srows)] = band_ref[g].astype(F32)
    brows = band_rows.shape[0]
    out_r, in_r = n_gx * lev_grp * trows, lev_grp * cy
    ri, rq = iota((out_r, brows), 0), iota((out_r, brows), 1)
    pick_r = (lax.div(ri, lev_grp * trows) == lax.div(rq, trows)) & (
        lax.rem(ri, trows) == lax.rem(rq, trows)
    )
    spread = jnp.dot(
        pick_r.astype(F32).astype(BF16), band_rows[...].astype(BF16), preferred_element_type=F32
    )
    cs, cc = iota((LANES, in_r), 0), iota((LANES, in_r), 1)
    pick_c = lax.rem(lax.rem(cc, cy), srows) == cs
    spread = jnp.dot(
        spread.astype(BF16), pick_c.astype(F32).astype(BF16), preferred_element_type=F32
    )
    ai, ac = iota((out_r, in_r), 0), iota((out_r, in_r), 1)
    keep = (lax.div(lax.rem(ai, lev_grp * trows), trows) == lax.div(ac, cy)) & (
        lax.div(lax.rem(ac, cy), srows) == lax.div(ai, lev_grp * trows)
    )
    band = jnp.where(keep, spread, 0.0).astype(BF16)

    number = gy * n_gx + gx
    ocean = jnp.ones((1, cx), F32)
    for i in range(land_ref.shape[0]):
        ocean = jnp.where(jnp.full((1, cx), land_ref[i], jnp.int32) == number, 0.0, ocean)

    wide = iota((cy, cx), 1)
    tall = iota((cy, cx), 0)
    has_above = jnp.where(gy < n_gy - 1, 1.0, 0.0).astype(F32)
    has_below = jnp.where(gy > 0, 1.0, 0.0).astype(F32)

    def advance(s, tiles, l):
        u = zonal[l].astype(F32) * (0.5 * ocean)
        v = merid[l].astype(F32) * (0.5 * ocean)
        kap = kappa_ref[l] * ocean
        own = 1.0 - 4.0 * kap
        results = []
        for t in range(2):
            k = t * levels + l
            c = tiles[t, l]
            e = jnp.where(
                wide == cx - 1, col_recv[s, 0, :, pl.ds(k, 1)], pltpu.roll(c, cx - 1, 1)
            )
            w = jnp.where(wide == 0, col_recv[s, 1, :, pl.ds(k, 1)], pltpu.roll(c, 1, 1))
            n = jnp.where(
                tall == cy - 1,
                row_recv[s, 0, t, pl.ds(l, 1), :] * has_above,
                pltpu.roll(c, cy - 1, 0),
            )
            b = jnp.where(
                tall == 0, row_recv[s, 1, t, pl.ds(l, 1), :] * has_below, pltpu.roll(c, 1, 0)
            )
            results.append(
                own * c + (kap * (e + w + n + b) - u * (e - w) - v * (n - b))
            )
        return results

    loads[2].wait()
    loads[3].wait()
    for copy in halo0:
        copy.wait()
    for l in range(levels):
        new = advance(0, x0, l)
        for t in range(2):
            x1[t, l] = new[t]
            pack_rows(1, t, l, new[t][:1], new[t][cy - 1 :])
    pack_columns(1, x1)
    halo1 = halo_copies(1)
    for copy in halo1:
        copy.start()

    for copy in halo1:
        copy.wait()

    mine = pl.multiple_of(gx * cx, LANES)
    exchanges = []
    local = []
    for h in range(halves):
        for l in range(h * lev_grp, (h + 1) * lev_grp):
            new = advance(1, x1, l)
            lev = (role * levels + l).astype(F32)
            factor = 0.17 * (1.0 + 0.03 * lev)
            t1, s1 = x1[0, l], x1[1, l]
            t2, s2 = new
            r1 = 0.78 * s1 - factor * t1 - 0.02 * t1 * t1
            r2 = 0.78 * s2 - factor * t2 - 0.02 * t2 * t2
            means[0, l] = (0.5 * (t1 + t2)).astype(BF16)
            means[1, l] = (0.5 * (s1 + s2)).astype(BF16)
            means[2, l] = (0.5 * (r1 + r2)).astype(BF16)
        for f in range(3):
            rows = means[f, pl.ds(h * lev_grp, lev_grp)].reshape(in_r, cx)
            lat = jnp.dot(band, rows, preferred_element_type=F32).astype(BF16)
            for g in range(n_gx):
                lat_send[g, f, h] = lat[g * 16 : (g + 1) * 16]
        for d in range(1, n_gx):
            target = wrap(gx + d, n_gx)
            copy = pltpu.make_async_remote_copy(
                src_ref=lat_send.at[target, :, h],
                dst_ref=lat_recv.at[:, h, :, pl.ds(mine, cx)],
                send_sem=a2a_send_sems.at[h, d],
                recv_sem=a2a_recv_sems.at[h, d],
                device_id=(role, gy, target),
                device_id_type=MESH,
            )
            copy.start()
            exchanges.append((h, copy))
        copy = pltpu.make_async_copy(
            lat_send.at[gx, :, h], lat_recv.at[:, h, :, pl.ds(mine, cx)], local_sems.at[h]
        )
        copy.start()
        local.append(copy)

    stores = []
    for h in range(halves):
        for when, copy in exchanges:
            if when == h:
                copy.wait_recv()
        local[h].wait()
        store = pltpu.make_async_copy(lat_recv.at[:, h], lat_out.at[:, h], out_sems.at[h])
        store.start()
        stores.append(store)
    for _, copy in exchanges:
        copy.wait_send()
    for store in stores:
        store.wait()


def remap_kernel(
    dims,
    lat_hbm,
    panel_hbm,
    start_ref,
    cluster_ref,
    area_ref,
    out_ref,
    part_ref,
    lat,
    wide,
    result,
    panel,
    sems,
):
    n_role, n_gy, n_gx, levels, cy, cx, trows, srows, nblk, sw, tb, groups = dims
    role, gy, gx = (lax.axis_index(a) for a in ("role", "gy", "gx"))
    lat_load = pltpu.make_async_copy(lat_hbm, lat, sems.at[nblk])
    lat_load.start()
    loads = [
        pltpu.make_async_copy(panel_hbm.at[j], panel.at[j], sems.at[j]) for j in range(nblk)
    ]
    for load in loads:
        load.start()

    glanes = part_ref.shape[1]
    lanes = iota((1, glanes), 1)
    labels = lax.rem(lanes, groups)

    def add_area(r, so_far):
        return so_far + jnp.where(labels == cluster_ref[r], area_ref[r], 0.0)

    zero = jnp.zeros((1, glanes), F32)
    all_rows = cluster_ref.shape[0]
    area_sum = lax.fori_loop(0, all_rows, add_area, zero, unroll=8)
    thick_total = sum(1.0 + 0.25 * k for k in range(levels * n_role))
    denom = area_sum * (thick_total * nblk * tb)

    first_row = (gy * n_gx + gx) * trows
    out_rows = 3 * levels * trows
    row = iota((out_rows, 1), 0)
    ti = lax.rem(row, trows)
    hot = jnp.zeros((out_rows, glanes), F32)
    for t in range(trows):
        row_hot = jnp.where(labels == cluster_ref[first_row + t], area_ref[first_row + t], 0.0)
        hot = jnp.where(ti == t, row_hot, hot)
    level = role * levels + lax.rem(lax.div(row, trows), levels)
    thick = 1.0 + 0.25 * level.astype(F32)

    lat_load.wait()
    columns = n_gx * cx
    wide[:, pl.ds(0, columns)] = lat[...].astype(F32)
    wide[:, pl.ds(columns, LANES)] = jnp.zeros((out_rows, LANES), F32)
    lane = iota((out_rows, LANES), 1)
    squares = jnp.zeros((out_rows, tb), F32)
    for j in range(nblk):
        start = start_ref[j]
        base = lax.div(start, LANES) * LANES
        shift = LANES - (start - base)
        turned = []
        for i in range(sw // LANES + 1):
            tile = wide[:, pl.ds(pl.multiple_of(base + i * LANES, LANES), LANES)]
            turned.append(pltpu.roll(tile, lax.rem(shift, LANES), 1))
        window = jnp.concatenate(
            [
                jnp.where(lane < shift, turned[i], turned[i + 1]).astype(BF16)
                for i in range(sw // LANES)
            ],
            axis=1,
        )
        loads[j].wait()
        values = jnp.dot(window, panel[j], preferred_element_type=F32)
        squares = squares + values * values
        result[:, pl.ds(j * tb, tb)] = values
    for i in range(3 * levels):
        out_ref[i // levels, i % levels] = result[pl.ds(i * trows, trows), :].astype(BF16)
    weighted = jnp.sum(squares, axis=1, keepdims=True) * thick * hot
    size = levels * trows
    field = lax.div(lanes, groups)
    numer = jnp.zeros((1, glanes), F32)
    for f in range(3):
        own = jnp.sum(weighted[f * size : (f + 1) * size], axis=0, keepdims=True)
        numer = jnp.where(field == f, own, numer)
    part_ref[...] = numer / denom


def sums_kernel(dims, part_ref, sums_ref, gather, sum_sems):
    n_role, n_gy, n_gx = dims[:3]
    role, gy, gx = (lax.axis_index(a) for a in ("role", "gy", "gx"))
    total = n_role * n_gy * n_gx
    me = (role * n_gy + gy) * n_gx + gx
    barrier = pltpu.get_barrier_semaphore()

    def for_others(do):
        if total <= 64:
            for d in range(1, total):
                do(peer_of(dims, d))
        else:

            @pl.loop(1, total)
            def _(d):
                do(peer_of(dims, d))

    def greet(device):
        pl.semaphore_signal(barrier, inc=1, device_id=device, device_id_type=MESH)

    def send(device):
        pltpu.make_async_remote_copy(
            src_ref=gather.at[me],
            dst_ref=gather.at[me],
            send_sem=sum_sems.at[0],
            recv_sem=sum_sems.at[1],
            device_id=device,
            device_id_type=MESH,
        ).start()

    for_others(greet)
    gather[me] = part_ref[...]
    pl.semaphore_wait(barrier, total - 1)
    for_others(send)
    every = gather.at[pl.ds(0, total - 1)]
    for i in (1, 0):
        pltpu.make_async_copy(every, every, sum_sems.at[i]).wait()
    sums_ref[...] = jnp.sum(gather[...], axis=0)


def body(
    dims,
    area,
    thermal_anomaly,
    saltiness_anomaly,
    zonal_flow_fraction,
    meridional_flow_fraction,
    mixing_coefficient,
    continent_patch_numbering,
    parallel_band_coefficients,
    meridian_panel_coefficients,
    panel_starting_source_meridian,
    target_parallel_cluster,
):
    n_role, n_gy, n_gx, levels, cy, cx, trows, srows, nblk, sw, tb, groups = dims
    total = n_role * n_gy * n_gx
    lev_grp = 16 // trows
    halves = levels // lev_grp
    glanes = -(-3 * groups // LANES) * LANES
    hbm = pl.BlockSpec(memory_space=pl.ANY)
    smem = pl.BlockSpec(memory_space=pltpu.SMEM)
    vmem = pl.BlockSpec(memory_space=pltpu.VMEM)
    brows = -(-n_gx * trows // LANES) * LANES
    dma = pltpu.SemaphoreType.DMA
    mib = 1024 * 1024
    lat = pl.pallas_call(
        functools.partial(model_kernel, dims),
        out_shape=jax.ShapeDtypeStruct((3, halves, 16, n_gx * cx), BF16),
        in_specs=[hbm] * 4 + [smem, smem, vmem],
        out_specs=hbm,
        scratch_shapes=[
            pltpu.VMEM((2, levels, cy, cx), F32),
            pltpu.VMEM((2, levels, cy, cx), F32),
            pltpu.VMEM((levels, cy, cx), BF16),
            pltpu.VMEM((levels, cy, cx), BF16),
            pltpu.VMEM((brows, LANES), F32),
            pltpu.VMEM((3, levels, cy, cx), BF16),
            pltpu.VMEM((n_gx, 3, halves, 16, cx), BF16),
            pltpu.VMEM((3, halves, 16, n_gx * cx), BF16),
            pltpu.VMEM((2, 2, 2, levels, cx), F32),
            pltpu.VMEM((2, 2, 2, levels, cx), F32),
            pltpu.VMEM((2, 2, cy, LANES), F32),
            pltpu.VMEM((2, 2, cy, LANES), F32),
            dma((4,)),
            dma((2, 4)),
            dma((2, 4)),
            dma((halves, n_gx)),
            dma((halves, n_gx)),
            dma((halves,)),
            dma((halves,)),
        ],
        compiler_params=pltpu.CompilerParams(
            collective_id=0, has_side_effects=True, vmem_limit_bytes=60 * mib
        ),
        name="model",
    )(
        thermal_anomaly,
        saltiness_anomaly,
        zonal_flow_fraction,
        meridional_flow_fraction,
        mixing_coefficient,
        continent_patch_numbering,
        parallel_band_coefficients,
    )
    out_rows = 3 * levels * trows
    remapped, part = pl.pallas_call(
        functools.partial(remap_kernel, dims),
        out_shape=(
            jax.ShapeDtypeStruct((3, levels, trows, nblk * tb), BF16),
            jax.ShapeDtypeStruct((1, glanes), F32),
        ),
        in_specs=[hbm, hbm, smem, smem, smem],
        out_specs=(vmem, vmem),
        scratch_shapes=[
            pltpu.VMEM((out_rows, n_gx * cx), BF16),
            pltpu.VMEM((out_rows, n_gx * cx + LANES), F32),
            pltpu.VMEM((out_rows, nblk * tb), F32),
            pltpu.VMEM((nblk, sw, tb), BF16),
            dma((nblk + 1,)),
        ],
        compiler_params=pltpu.CompilerParams(vmem_limit_bytes=60 * mib),
        name="remap",
    )(
        lat.reshape(out_rows, n_gx * cx),
        meridian_panel_coefficients,
        panel_starting_source_meridian,
        target_parallel_cluster,
        jnp.asarray(area),
    )
    sums = pl.pallas_call(
        functools.partial(sums_kernel, dims),
        out_shape=jax.ShapeDtypeStruct((1, glanes), F32),
        in_specs=[vmem],
        out_specs=vmem,
        scratch_shapes=[pltpu.VMEM((total, 1, glanes), F32), dma((2,))],
        compiler_params=pltpu.CompilerParams(
            collective_id=1, has_side_effects=True, vmem_limit_bytes=16 * mib
        ),
        name="sums",
    )(part)
    return remapped, sums[0, : 3 * groups].reshape(3, groups)


def solution(mesh):
    in_specs = (
        P("role", "gy", "gx"),
        P("role", "gy", "gx"),
        P("role", "gy", "gx"),
        P("role", "gy", "gx"),
        P("role"),
        P(),
        P("gy", None, None),
        P(),
        P(),
        P(),
    )
    out_specs = (P(None, "role", ("gy", "gx"), None), P())

    def run(*args):
        n_role, n_gy, n_gx = (mesh.shape[a] for a in ("role", "gy", "gx"))
        levels, rows, cols = args[0].shape
        _, trows, srows = args[6].shape
        nblk, sw, tb = args[7].shape
        dims = (
            n_role,
            n_gy,
            n_gx,
            levels // n_role,
            rows // n_gy,
            cols // n_gx,
            trows,
            srows,
            nblk,
            sw,
            tb,
            4 * n_gy,
        )
        nrows = args[9].shape[0]
        r = np.arange(nrows, dtype=np.float64)
        area = np.cos((-75.0 + 150.0 * (r + 0.5) / nrows) * (math.pi / 180.0)).astype(np.float32)
        return jax.shard_map(
            functools.partial(body, dims, area),
            mesh=mesh,
            in_specs=in_specs,
            out_specs=out_specs,
            check_vma=False,
        )(*args)

    return run
```

profile of v0, /device:TPU:0, one launch (start us, length us, event | category | flops | bytes accessed | tf_op | source)
XLA Modules:
  0.0 40.6 jit_solution(2436129987466775555)
XLA Ops:
  0.6 25.8 %model.1 = bf16[3,2,16,2048]{3,2,1,0:T(8,128)(2,1)} custom-call(f32[8,96,256]{2,1,0:T(8,128)} %temp_hbm.1, f32[8,96,256]{2,1,0:T(8,128)} %salt_hbm.1, bf16[8,96,256]{2,1,0:T(8,128)(2,1)} %zonal_hbm.1, bf16[8,96,256]{2,1,0:T(8,128)(2,1)} %merid_hbm.1, f32[8]{0:T(128)} %kappa_ref.1, s32[2]{0:T(128)} %land_ref.1, bf16[8,4,12]{2,1,0:T(4,128)(2,1)} %band_ref.1), custom_call_target="tpu_custom_call" | custom-call | tf_op jit(solution)/shard_map/model/pallas_call | solution.py:422
  26.5 5.2 %remap.1 = (bf16[3,8,4,1792]{3,2,1,0:T(4,128)(2,1)}, f32[1,128]{1,0:T(1,128)}) custom-call(bf16[96,2048]{1,0:T(8,128)(2,1)} %bitcast.1, bf16[14,512,128]{2,1,0:T(8,128)(2,1)} %panel_hbm.1, s32[14]{0:T(128)} %start_ref.1, s32[64]{0:T(128)} %cluster_ref.1, f32[64]{0:T(128)} %constant.2.clone.area_ref), custom_call_target="tpu_custom_call" | custom-call | tf_op jit(solution)/shard_map/remap/pallas_call | solution.py:462
  31.7 0.0 copy-start
  31.7 0.6 %copy-done = f32[1,128]{1,0:T(1,128)S(1)} copy-done((f32[1,128]{1,0:T(1,128)S(1)}, f32[1,128]{1,0:T(1,128)}, u32[]{:S(2)}) %copy-start) | copy-done | bytes 536
  32.4 7.6 %sums.1 = f32[1,128]{1,0:T(1,128)S(1)} custom-call(f32[1,128]{1,0:T(1,128)S(1)} %copy-done), custom_call_target="tpu_custom_call" | custom-call | tf_op jit(solution)/shard_map/sums/pallas_call | solution.py:486
  39.9 0.7 %reshape_squeeze.3 = f32[3,8]{1,0:T(4,128)} reshape(f32[24]{0:T(128)S(1)} %slice_reduce_fusion) | data formatting | bytes 192 | tf_op jit(solution)/shard_map/reshape;squeeze | solution.py:497
  (1 shorter events, 0.0 us)
Async XLA Ops:
  31.7 0.7 %copy-start = (f32[1,128]{1,0:T(1,128)S(1)}, f32[1,128]{1,0:T(1,128)}, u32[]{:S(2)}) copy-start(f32[1,128]{1,0:T(1,128)} %get-tuple-element.5.part_ref) | copy-start | bytes 1540
where the time goes:
time: 40.9 us; the launch traced here: 40.6 us
  Pallas kernels  38.6 us (94%)
  local copies, waits for them, and re-layouts  1.33 us (3%)
  between operations  0.66 us (2%)
    pallas_call x1, Pallas kernels, body(): pl.pallas_call(functools.partial(model_kernel, dims), out_shape=jax.Shape...  25.8 us
    pallas_call x1, Pallas kernels, body(): pl.pallas_call(functools.partial(sums_kernel, dims), out_shape=jax.ShapeD...  7.57 us
    pallas_call x1, Pallas kernels, body(): pl.pallas_call(functools.partial(remap_kernel, dims), out_shape=(jax.Shap...  5.21 us

commit v1 on v0

v1 whole, which is shorter than its diff:
```python
import functools
import math

import jax
import jax.numpy as jnp
import numpy as np
from jax import lax
from jax.experimental import pallas as pl
from jax.experimental.pallas import tpu as pltpu
from jax.sharding import PartitionSpec as P

LANES = 128
SUB = 8
EDGE = 4
F32 = jnp.float32
BF16 = jnp.bfloat16
MESH = pl.DeviceIdType.MESH


def wrap(value, count):
    return jnp.where(value >= count, value - count, value)


def iota(shape, dim):
    return lax.broadcasted_iota(jnp.int32, shape, dim)


def turn(value, shift, axis):
    size = value.shape[axis]
    shift = shift % size
    return pltpu.roll(value, shift, axis) if shift else value


def position():
    return tuple(lax.axis_index(a) for a in ("role", "gy", "gx"))


def peer_of(dims, d):
    n_role, n_gy, n_gx = dims[:3]
    role, gy, gx = position()
    dx, dyr = d % n_gx, d // n_gx
    dy, dr = dyr % n_gy, dyr // n_gy
    return (wrap(role + dr, n_role), wrap(gy + dy, n_gy), wrap(gx + dx, n_gx))


def kernel(
    dims,
    temp_hbm,
    salt_hbm,
    zonal_hbm,
    merid_hbm,
    panel_hbm,
    kappa_ref,
    land_ref,
    start_ref,
    cluster_ref,
    area_ref,
    band_ref,
    out_hbm,
    sums_ref,
    x0,
    x1,
    uv,
    means,
    halo_x,
    halo_uv,
    cols,
    band_rows,
    lat_send,
    lat,
    e_send,
    e_recv,
    placed,
    panel,
    shifted,
    result,
    out_vmem,
    gather,
    in_sems,
    panel_sems,
    halo_send_sems,
    halo_recv_sems,
    a2a_send_sems,
    a2a_recv_sems,
    local_sems,
    e_send_sems,
    e_recv_sems,
    sum_sems,
    out_sem,
):
    n_role, n_gy, n_gx, levels, cy, cx, trows, srows, nblk, sw, tb, groups = dims
    role, gy, gx = position()
    total = n_role * n_gy * n_gx
    me = (role * n_gy + gy) * n_gx + gx
    lev_grp = 16 // trows
    halves = levels // lev_grp
    lev_rows = lev_grp * trows
    half_rows = 3 * lev_rows
    nk = EDGE * levels
    peer = functools.partial(peer_of, dims)

    sources = ((temp_hbm, x0.at[0]), (salt_hbm, x0.at[1]), (zonal_hbm, uv.at[0]), (merid_hbm, uv.at[1]))
    loads = [pltpu.make_async_copy(src, dst, in_sems.at[i]) for i, (src, dst) in enumerate(sources)]
    for load in loads:
        load.start()
    panel_loads = [
        pltpu.make_async_copy(panel_hbm.at[j], panel.at[j], panel_sems.at[j]) for j in range(nblk)
    ]
    for load in panel_loads:
        load.start()

    barrier = pltpu.get_barrier_semaphore()
    greeted = set(range(1, n_gx)) | {d * n_gx for d in range(1, n_role * n_gy)}
    for dy in {1, n_gy - 1}:
        for dx in {1, n_gx - 1}:
            greeted.add(dy * n_gx + dx)
    greeted = sorted(greeted)
    for d in greeted:
        pl.semaphore_signal(barrier, inc=1, device_id=peer(d), device_id_type=MESH)

    has_below = gy > 0
    has_above = gy < n_gy - 1

    @pl.when(gy == 0)
    def _():
        halo_x[0] = jnp.zeros_like(halo_x[0])
        halo_uv[0] = jnp.zeros_like(halo_uv[0])
        for i in range(4):
            cols[i, pl.ds(0, SUB)] = jnp.zeros((SUB, LANES), F32)

    @pl.when(gy == n_gy - 1)
    def _():
        halo_x[1] = jnp.zeros_like(halo_x[1])
        halo_uv[1] = jnp.zeros_like(halo_uv[1])
        for i in range(4):
            cols[i, pl.ds(SUB + cy, SUB)] = jnp.zeros((SUB, LANES), F32)

    columns = n_gx * cx
    lat[columns // LANES] = jnp.zeros((halves * half_rows, LANES), BF16)

    def ocean_of(dy, dx):
        ty = gy + dy
        tx = wrap(gx + dx + n_gx, n_gx)
        number = jnp.full((1, cx), ty * n_gx + tx, jnp.int32)
        flag = jnp.where((jnp.full((1, cx), ty, jnp.int32) >= 0) & (jnp.full((1, cx), ty, jnp.int32) < n_gy), 1.0, 0.0)
        for i in range(land_ref.shape[0]):
            flag = jnp.where(jnp.full((1, cx), land_ref[i], jnp.int32) == number, 0.0, flag)
        return flag

    ocean = ocean_of(0, 0)

    band_rows[...] = jnp.zeros_like(band_rows)
    for g in range(n_gx):
        band_rows[pl.ds(g * trows, trows), pl.ds(0, srows)] = band_ref[g].astype(F32)
    brows = band_rows.shape[0]
    out_r, in_r = n_gx * lev_rows, lev_grp * cy
    flat = band_rows[...].astype(BF16)
    ri, rq = iota((out_r, brows), 0), iota((out_r, brows), 1)
    pick_r = (lax.div(ri, lev_rows) == lax.div(rq, trows)) & (
        lax.rem(ri, trows) == lax.rem(rq, trows)
    )
    spread = jnp.dot(pick_r.astype(F32).astype(BF16), flat, preferred_element_type=F32)
    cs, cc = iota((LANES, in_r), 0), iota((LANES, in_r), 1)
    pick_c = (lax.rem(lax.rem(cc, cy), srows) == cs).astype(F32).astype(BF16)
    spread = jnp.dot(spread.astype(BF16), pick_c, preferred_element_type=F32)
    ai, ac = iota((out_r, in_r), 0), iota((out_r, in_r), 1)
    keep = (lax.div(lax.rem(ai, lev_rows), trows) == lax.div(ac, cy)) & (
        lax.div(lax.rem(ac, cy), srows) == lax.div(ai, lev_rows)
    )
    band = jnp.where(keep, spread, 0.0).astype(BF16)

    lane = iota((1, LANES), 1)
    quad = lax.div(lane, EDGE)
    col = lax.rem(lane, EDGE)

    for load in loads:
        load.wait()
    first = jnp.zeros((cy, LANES), F32)
    last = jnp.zeros((cy, LANES), F32)
    for q in range(4 * levels):
        kind, l = q // levels, q % levels
        source = x0.at[kind, l] if kind < 2 else uv.at[kind - 2, l]
        head = source[:, pl.ds(0, LANES)].astype(F32)
        tail = source[:, pl.ds(cx - LANES, LANES)].astype(F32)
        first = jnp.where(quad == q, turn(head, EDGE * q, 1), first)
        last = jnp.where(quad == q, turn(tail, EDGE * (q + 1), 1), last)
    cols[1, pl.ds(SUB, cy)] = first
    cols[2, pl.ds(SUB, cy)] = last

    west = wrap(gx + n_gx - 1, n_gx)
    east = wrap(gx + 1, n_gx)
    own_w, own_e = cols.at[1, pl.ds(SUB, cy)], cols.at[2, pl.ds(SUB, cy)]
    plan = [
        (None, None, own_w, cols.at[3, pl.ds(SUB, cy)], (role, gy, west)),
        (None, None, own_e, cols.at[0, pl.ds(SUB, cy)], (role, gy, east)),
    ]
    for side, (can_send, can_recv) in enumerate(((has_below, has_above), (has_above, has_below))):
        ty = gy - 1 if side == 0 else gy + 1
        mine = SUB if side == 0 else cy
        theirs = SUB + cy if side == 0 else 0
        for block, there, tx in ((1, 1, gx), (2, 2, gx), (1, 3, west), (2, 0, east)):
            plan.append(
                (
                    can_send,
                    can_recv,
                    cols.at[block, pl.ds(mine, SUB)],
                    cols.at[there, pl.ds(theirs, SUB)],
                    (role, ty, tx),
                )
            )
        row = 0 if side == 0 else cy - 2
        slot = 0 if side == 0 else SUB - 2
        for t, ref in enumerate((temp_hbm, salt_hbm)):
            plan.append(
                (
                    can_send,
                    can_recv,
                    ref.at[:, pl.ds(row, 2), :],
                    halo_x.at[1 - side, t, :, pl.ds(slot, 2), :],
                    (role, ty, gx),
                )
            )
        row = 0 if side == 0 else cy - SUB
        for t, ref in enumerate((zonal_hbm, merid_hbm)):
            plan.append(
                (
                    can_send,
                    can_recv,
                    ref.at[:, pl.ds(row, SUB), :],
                    halo_uv.at[1 - side, t],
                    (role, ty, gx),
                )
            )

    def when(cond, do):
        if cond is None:
            do()
        else:
            pl.when(cond)(do)

    halos = []
    for i, (can_send, can_recv, src, dst, target) in enumerate(plan):
        copy = pltpu.make_async_remote_copy(
            src_ref=src,
            dst_ref=dst,
            send_sem=halo_send_sems.at[i],
            recv_sem=halo_recv_sems.at[i],
            device_id=target,
            device_id_type=MESH,
        )
        halos.append((can_send, can_recv, copy))
    column_halos = halos[:2] + halos[2:6] + halos[10:14]
    row_halos = halos[6:10] + halos[14:18]

    pl.semaphore_wait(barrier, len(greeted))
    for can_send, _, copy in halos:
        when(can_send, copy.start)

    level0 = role * levels

    def advance(c, e, w, n, b, u, v, kap):
        return (1.0 - 4.0 * kap) * c + (kap * (e + w + n + b) - u * (e - w) - v * (n - b))

    def whole(c, u, v, kap):
        return advance(
            c, turn(c, -1, 1), turn(c, 1, 1), turn(c, -1, 0), turn(c, 1, 0), u, v, kap
        )

    def density(temp, salt, factor):
        return 0.78 * salt - factor * temp - 0.02 * temp * temp

    def factor_of(l):
        return 0.17 * (1.0 + 0.03 * (level0 + l).astype(F32))

    wide = iota((1, cx), 1)
    at_edge = (wide < 2) | (wide >= cx - 2)
    tiles = cx // LANES
    order = sorted(range(1, n_gx), key=lambda d: -min(d, n_gx - d))
    at_end = (gx == 0) | (gx == n_gx - 1)

    def bulk(h, d):
        target = wrap(gx + d, n_gx)
        return target, pltpu.make_async_remote_copy(
            src_ref=lat_send.at[h, target],
            dst_ref=lat.at[pl.ds(gx * tiles, tiles), pl.ds(h * half_rows, half_rows)],
            send_sem=a2a_send_sems.at[h, d],
            recv_sem=a2a_recv_sems.at[h, d],
            device_id=(role, gy, target),
            device_id_type=MESH,
        )

    def local(h):
        return pltpu.make_async_copy(
            lat_send.at[h, gx],
            lat.at[pl.ds(gx * tiles, tiles), pl.ds(h * half_rows, half_rows)],
            local_sems.at[h],
        )

    def stage(h, g, f, rows):
        for i in range(tiles):
            lat_send[h, g, i, pl.ds(f * lev_rows, lev_rows)] = rows[
                :, i * LANES : (i + 1) * LANES
            ]

    for h in range(halves):
        for l in range(h * lev_grp, (h + 1) * lev_grp):
            u = uv[0, l].astype(F32) * (0.5 * ocean)
            v = uv[1, l].astype(F32) * (0.5 * ocean)
            kap = kappa_ref[l] * ocean
            one = [whole(x0[t, l], u, v, kap) for t in range(2)]
            two = [whole(one[t], u, v, kap) for t in range(2)]
            factor = factor_of(l)
            r1 = density(one[0], one[1], factor)
            r2 = density(two[0], two[1], factor)
            x1[0, l] = one[0]
            x1[1, l] = one[1]
            means[0, l] = (0.5 * (one[0] + two[0])).astype(BF16)
            means[1, l] = (0.5 * (one[1] + two[1])).astype(BF16)
            means[2, l] = (0.5 * (r1 + r2)).astype(BF16)
        for f in range(3):
            rows = means[f, pl.ds(h * lev_grp, lev_grp)].reshape(in_r, cx)
            got = jnp.dot(
                band[lev_rows : out_r - lev_rows], rows, preferred_element_type=F32
            )
            got = jnp.where(at_edge, 0.0, got).astype(BF16)
            for g in range(1, n_gx - 1):
                stage(h, g, f, got[(g - 1) * lev_rows : g * lev_rows])
        for d in order:
            target, copy = bulk(h, d)
            pl.when((target > 0) & (target < n_gx - 1))(copy.start)
        pl.when(jnp.logical_not(at_end))(local(h).start)

    for _, can_recv, copy in column_halos:
        when(can_recv, copy.wait_recv)
    cye = cy + 2 * SUB
    row_e = iota((cye, 1), 0)
    kap_l = jnp.zeros((1, LANES), F32)
    factor_l = jnp.zeros((1, LANES), F32)
    lane_level = lax.div(lax.rem(lane, nk), EDGE)
    for l in range(levels):
        kap_l = jnp.where(lane_level == l, kappa_ref[l], kap_l)
        factor_l = jnp.where(lane_level == l, factor_of(l), factor_l)

    flags = {(dy, dx): ocean_of(dy, dx)[:, :LANES] for dy in (-1, 0, 1) for dx in (-1, 0, 1)}

    def coefficients(i, dx):
        block = cols[i]
        oc = jnp.where(
            row_e < SUB, flags[-1, dx], jnp.where(row_e < SUB + cy, flags[0, dx], flags[1, dx])
        )
        half = 0.5 * oc
        u = jnp.where(lane < nk, turn(block, -2 * nk, 1), turn(block, -nk, 1)) * half
        v = jnp.where(lane < nk, turn(block, -3 * nk, 1), turn(block, -2 * nk, 1)) * half
        return u, v, kap_l * oc

    def step_left(left, right, coef):
        e = jnp.where(col == EDGE - 1, turn(right, EDGE - 1, 1), turn(left, -1, 1))
        return advance(left, e, turn(left, 1, 1), turn(left, -1, 0), turn(left, 1, 0), *coef)

    def step_right(left, right, coef):
        w = jnp.where(col == 0, turn(left, 1 - EDGE, 1), turn(right, 1, 1))
        return advance(
            right, turn(right, -1, 1), w, turn(right, -1, 0), turn(right, 1, 0), *coef
        )

    own = coefficients(1, 0)
    left1 = step_left(cols[0], cols[1], coefficients(0, -1))
    west1 = step_right(cols[0], cols[1], own)
    west2 = step_right(left1, west1, own)
    own = coefficients(2, 0)
    east1 = step_left(cols[2], cols[3], own)
    right1 = step_right(cols[2], cols[3], coefficients(3, 1))
    east2 = step_left(east1, right1, own)
    both1 = jnp.where(col < 2, west1, east1)[SUB : SUB + cy]
    both2 = jnp.where(col < 2, west2, east2)[SUB : SUB + cy]
    rho = 0.5 * (
        density(both1, turn(both1, -nk, 1), factor_l)
        + density(both2, turn(both2, -nk, 1), factor_l)
    )
    packed = jnp.where(
        lane < 2 * nk,
        0.5 * (both1 + both2),
        jnp.where(lane < 3 * nk, turn(rho, 2 * nk, 1), 0.0),
    ).astype(BF16)
    narrow = n_gx * trows
    thin = jnp.dot(flat[:narrow], pick_c[:, :cy], preferred_element_type=F32)
    ei, ec = iota((narrow, cy), 0), iota((narrow, cy), 1)
    thin = jnp.where(lax.div(ec, srows) == lax.div(ei, trows), thin, 0.0).astype(BF16)
    edge_lat = jnp.dot(thin, packed, preferred_element_type=F32).astype(BF16)
    for g in range(n_gx):
        e_send[g] = edge_lat[g * trows : (g + 1) * trows]

    e_copies = []
    for d in order:
        target = wrap(gx + d, n_gx)
        copy = pltpu.make_async_remote_copy(
            src_ref=e_send.at[target],
            dst_ref=e_recv.at[gx],
            send_sem=e_send_sems.at[d],
            recv_sem=e_recv_sems.at[d],
            device_id=(role, gy, target),
            device_id_type=MESH,
        )
        copy.start()
        e_copies.append(copy)
    e_recv[pl.ds(gx, 1)] = e_send[pl.ds(gx, 1)]

    for _, can_recv, copy in row_halos:
        when(can_recv, copy.wait_recv)
    sub8 = iota((SUB, 1), 0)
    ocean_below, ocean_above = ocean_of(-1, 0), ocean_of(1, 0)

    def up(a, b):
        return jnp.where(sub8 == SUB - 1, turn(b, -1, 0), turn(a, -1, 0))

    def down(a, b):
        return jnp.where(sub8 == 0, turn(a, 1, 0), turn(b, 1, 0))

    def rows_step(c, n, b, u, v, kap):
        return advance(c, turn(c, -1, 1), turn(c, 1, 1), n, b, u, v, kap)

    for l in range(levels):
        kap = kappa_ref[l] * ocean
        factor = factor_of(l)
        flow = [uv[i, l, pl.ds(0, 16)].astype(F32)[:SUB] * (0.5 * ocean) for i in range(2)]
        other = [halo_uv[0, i, l].astype(F32) * (0.5 * ocean_below) for i in range(2)]
        kap_o = kappa_ref[l] * ocean_below
        ones, twos = [], []
        for t in range(2):
            far, edge, near = halo_x[0, t, l], x0[t, l, pl.ds(0, SUB)], x0[t, l, pl.ds(SUB, SUB)]
            out1 = rows_step(far, up(far, edge), turn(far, 1, 0), *other, kap_o)
            in1 = rows_step(edge, up(edge, near), down(far, edge), *flow, kap)
            ones.append(in1)
            next1 = x1[t, l, pl.ds(SUB, SUB)]
            twos.append(rows_step(in1, up(in1, next1), down(out1, in1), *flow, kap))
        r = density(*ones, factor) + density(*twos, factor)
        for f, value in enumerate((ones[0] + twos[0], ones[1] + twos[1], r)):
            means[f, l, pl.ds(0, SUB)] = (0.5 * value).astype(BF16)

        flow = [uv[i, l, pl.ds(cy - 16, 16)].astype(F32)[SUB:] * (0.5 * ocean) for i in range(2)]
        other = [halo_uv[1, i, l].astype(F32) * (0.5 * ocean_above) for i in range(2)]
        kap_o = kappa_ref[l] * ocean_above
        ones, twos = [], []
        for t in range(2):
            far = halo_x[1, t, l]
            edge = x0[t, l, pl.ds(cy - SUB, SUB)]
            near = x0[t, l, pl.ds(cy - 2 * SUB, SUB)]
            out1 = rows_step(far, turn(far, -1, 0), down(edge, far), *other, kap_o)
            in1 = rows_step(edge, up(edge, far), down(near, edge), *flow, kap)
            ones.append(in1)
            next1 = x1[t, l, pl.ds(cy - 2 * SUB, SUB)]
            twos.append(rows_step(in1, up(in1, out1), down(next1, in1), *flow, kap))
        r = density(*ones, factor) + density(*twos, factor)
        for f, value in enumerate((ones[0] + twos[0], ones[1] + twos[1], r)):
            means[f, l, pl.ds(cy - SUB, SUB)] = (0.5 * value).astype(BF16)

    ends = jnp.concatenate([band[:lev_rows], band[out_r - lev_rows :]], axis=0)
    for h in range(halves):
        for f in range(3):
            rows = means[f, pl.ds(h * lev_grp, lev_grp)].reshape(in_r, cx)
            got = jnp.dot(ends, rows, preferred_element_type=F32)
            got = jnp.where(at_edge, 0.0, got).astype(BF16)
            stage(h, 0, f, got[:lev_rows])
            stage(h, n_gx - 1, f, got[lev_rows:])
        for d in order:
            target, copy = bulk(h, d)
            pl.when((target == 0) | (target == n_gx - 1))(copy.start)
        pl.when(at_end)(local(h).start)

    depth = sw + LANES
    sub = iota((1, SUB, 1), 1)

    def tile_of(j):
        return lax.div(start_ref[j], LANES)

    blank = jnp.zeros((SUB, tb), F32)
    for j in range(nblk):
        panel_loads[j].wait()
        off = jnp.full((1, tb), start_ref[j] - tile_of(j) * LANES, jnp.int32)
        rows = panel[j].astype(F32)
        parts = [rows[i * SUB : (i + 1) * SUB] for i in range(sw // SUB)]
        bit = 1
        while bit < SUB:
            taken = lax.rem(lax.div(off, bit), 2) == 1
            low = sub8 < bit
            ring = [turn(part, bit, 0) for part in parts] + [blank]
            parts = [
                jnp.where(
                    taken,
                    jnp.where(low, ring[i - 1] if i else blank, ring[i]),
                    parts[i] if i < len(parts) else blank,
                )
                for i in range(len(ring))
            ] if bit == 1 else [
                jnp.where(taken, jnp.where(low, ring[i - 1] if i else blank, ring[i]), parts[i])
                for i in range(len(parts))
            ]
            bit *= 2
        step = 1
        while step * SUB < LANES:
            taken = lax.rem(lax.div(off, step * SUB), 2) == 1
            longer = len(parts) + step
            parts = [
                jnp.where(
                    taken,
                    parts[i - step] if i >= step else blank,
                    parts[i] if i < len(parts) else blank,
                )
                for i in range(longer)
            ]
            step *= 2
        assert len(parts) == depth // SUB
        shifted[j] = jnp.concatenate(parts, axis=0).astype(BF16)

    glanes = gather.shape[2]
    lanes = iota((1, glanes), 1)
    labels = lax.rem(lanes, groups)

    def add_area(r, so_far):
        return so_far + jnp.where(labels == cluster_ref[r], area_ref[r], 0.0)

    area_sum = lax.fori_loop(
        0, cluster_ref.shape[0], add_area, jnp.zeros((1, glanes), F32), unroll=8
    )
    thick_total = sum(1.0 + 0.25 * k for k in range(levels * n_role))
    denom = area_sum * (thick_total * nblk * tb)
    first_row = (gy * n_gx + gx) * trows
    out_rows = halves * half_rows
    orow = iota((out_rows, 1), 0)
    ti = lax.rem(orow, trows)
    hot = jnp.zeros((out_rows, glanes), F32)
    for t in range(trows):
        row_hot = jnp.where(labels == cluster_ref[first_row + t], area_ref[first_row + t], 0.0)
        hot = jnp.where(ti == t, row_hot, hot)
    olevel = lax.div(orow, half_rows) * lev_grp + lax.div(lax.rem(orow, lev_rows), trows)
    ofield = lax.div(lax.rem(orow, half_rows), lev_rows)
    thick = 1.0 + 0.25 * (level0 + olevel).astype(F32)
    field = lax.div(lanes, groups)
    hot = jnp.where(ofield == field, hot * thick, 0.0)

    pk, pc = iota((LANES, cx), 0), iota((LANES, cx), 1)
    place = jnp.where(pc < 2, pc, jnp.where(pc >= cx - 2, pc - (cx - EDGE), -1))
    place = (place == lax.rem(pk, EDGE)).astype(F32).astype(BF16)
    mine_q = ofield * levels + olevel
    for copy in e_copies:
        copy.wait_recv()
    for s in range(n_gx):
        block = e_recv[s].astype(F32)
        tall = jnp.concatenate([block] * (out_rows // trows), axis=0)
        tall = jnp.where(quad == mine_q, tall, 0.0).astype(BF16)
        put = jnp.dot(tall, place, preferred_element_type=F32).astype(BF16)
        for i in range(tiles):
            placed[s * tiles + i] = put[:, i * LANES : (i + 1) * LANES]

    for h in range(halves):
        for d in order:
            bulk(h, d)[1].wait_recv()
        local(h).wait()
    for i in range(n_gx * tiles):
        lat[i] = lat[i] + placed[i]
    squares = jnp.zeros((out_rows, tb), F32)
    for j in range(nblk):
        tile = tile_of(j)
        window = jnp.concatenate([lat[tile + i] for i in range(depth // LANES)], axis=1)
        values = jnp.dot(window, shifted[j], preferred_element_type=F32)
        squares = squares + values * values
        result[:, pl.ds(j * tb, tb)] = values
    weighted = jnp.sum(squares, axis=1, keepdims=True) * hot
    part = jnp.sum(weighted, axis=0, keepdims=True) / denom

    def for_others(do):
        if total <= 64:
            for d in range(1, total):
                do(peer(d))
        else:

            @pl.loop(1, total)
            def _(d):
                do(peer(d))

    def send(device):
        pltpu.make_async_remote_copy(
            src_ref=gather.at[me],
            dst_ref=gather.at[me],
            send_sem=sum_sems.at[0],
            recv_sem=sum_sems.at[1],
            device_id=device,
            device_id_type=MESH,
        ).start()

    gather[me] = part
    for_others(send)

    for h in range(halves):
        for f in range(3):
            for i in range(lev_grp):
                row = h * half_rows + f * lev_rows + i * trows
                out_vmem[f, h * lev_grp + i] = result[pl.ds(row, trows), :].astype(BF16)
    store = pltpu.make_async_copy(out_vmem, out_hbm, out_sem)
    store.start()

    for can_send, _, copy in halos:
        when(can_send, copy.wait_send)
    for h in range(halves):
        for d in order:
            bulk(h, d)[1].wait_send()
    for copy in e_copies:
        copy.wait_send()
    store.wait()
    every = gather.at[pl.ds(0, total - 1)]
    for i in (1, 0):
        pltpu.make_async_copy(every, every, sum_sems.at[i]).wait()
    sums = jnp.sum(gather[...], axis=0)
    for f in range(3):
        sums_ref[pl.ds(f, 1), :] = turn(sums, -f * groups, 1)[:, :groups]


def body(
    dims,
    area,
    thermal_anomaly,
    saltiness_anomaly,
    zonal_flow_fraction,
    meridional_flow_fraction,
    mixing_coefficient,
    continent_patch_numbering,
    parallel_band_coefficients,
    meridian_panel_coefficients,
    panel_starting_source_meridian,
    target_parallel_cluster,
):
    n_role, n_gy, n_gx, levels, cy, cx, trows, srows, nblk, sw, tb, groups = dims
    total = n_role * n_gy * n_gx
    lev_grp = 16 // trows
    halves = levels // lev_grp
    half_rows = 3 * lev_grp * trows
    glanes = -(-3 * groups // LANES) * LANES
    hbm = pl.BlockSpec(memory_space=pl.ANY)
    smem = pl.BlockSpec(memory_space=pltpu.SMEM)
    vmem = pl.BlockSpec(memory_space=pltpu.VMEM)
    brows = -(-n_gx * trows // LANES) * LANES
    dma = pltpu.SemaphoreType.DMA
    columns = n_gx * cx
    out_rows = halves * half_rows
    return pl.pallas_call(
        functools.partial(kernel, dims),
        out_shape=(
            jax.ShapeDtypeStruct((3, levels, trows, nblk * tb), BF16),
            jax.ShapeDtypeStruct((3, groups), F32),
        ),
        in_specs=[hbm] * 5 + [smem] * 5 + [vmem],
        out_specs=(hbm, vmem),
        scratch_shapes=[
            pltpu.VMEM((2, levels, cy, cx), F32),
            pltpu.VMEM((2, levels, cy, cx), F32),
            pltpu.VMEM((2, levels, cy, cx), BF16),
            pltpu.VMEM((3, levels, cy, cx), BF16),
            pltpu.VMEM((2, 2, levels, SUB, cx), F32),
            pltpu.VMEM((2, 2, levels, SUB, cx), BF16),
            pltpu.VMEM((4, cy + 2 * SUB, LANES), F32),
            pltpu.VMEM((brows, LANES), F32),
            pltpu.VMEM((halves, n_gx, cx // LANES, half_rows, LANES), BF16),
            pltpu.VMEM((columns // LANES + 1, out_rows, LANES), BF16),
            pltpu.VMEM((n_gx, trows, LANES), BF16),
            pltpu.VMEM((n_gx, trows, LANES), BF16),
            pltpu.VMEM((columns // LANES, out_rows, LANES), BF16),
            pltpu.VMEM((nblk, sw, tb), BF16),
            pltpu.VMEM((nblk, sw + LANES, tb), BF16),
            pltpu.VMEM((out_rows, nblk * tb), F32),
            pltpu.VMEM((3, levels, trows, nblk * tb), BF16),
            pltpu.VMEM((total, 1, glanes), F32),
            dma((4,)),
            dma((nblk,)),
            dma((18,)),
            dma((18,)),
            dma((halves, n_gx)),
            dma((halves, n_gx)),
            dma((halves,)),
            dma((n_gx,)),
            dma((n_gx,)),
            dma((2,)),
            dma(()),
        ],
        compiler_params=pltpu.CompilerParams(
            collective_id=0, has_side_effects=True, vmem_limit_bytes=60 * 1024 * 1024
        ),
        name="ocean",
    )(
        thermal_anomaly,
        saltiness_anomaly,
        zonal_flow_fraction,
        meridional_flow_fraction,
        meridian_panel_coefficients,
        mixing_coefficient,
        continent_patch_numbering,
        panel_starting_source_meridian,
        target_parallel_cluster,
        jnp.asarray(area),
        parallel_band_coefficients,
    )


def solution(mesh):
    in_specs = (
        P("role", "gy", "gx"),
        P("role", "gy", "gx"),
        P("role", "gy", "gx"),
        P("role", "gy", "gx"),
        P("role"),
        P(),
        P("gy", None, None),
        P(),
        P(),
        P(),
    )
    out_specs = (P(None, "role", ("gy", "gx"), None), P())

    def run(*args):
        n_role, n_gy, n_gx = (mesh.shape[a] for a in ("role", "gy", "gx"))
        levels, rows, cols = args[0].shape
        _, trows, srows = args[6].shape
        nblk, sw, tb = args[7].shape
        dims = (
            n_role,
            n_gy,
            n_gx,
            levels // n_role,
            rows // n_gy,
            cols // n_gx,
            trows,
            srows,
            nblk,
            sw,
            tb,
            4 * n_gy,
        )
        nrows = args[9].shape[0]
        r = np.arange(nrows, dtype=np.float64)
        area = np.cos((-75.0 + 150.0 * (r + 0.5) / nrows) * (math.pi / 180.0)).astype(np.float32)
        return jax.shard_map(
            functools.partial(body, dims, area),
            mesh=mesh,
            in_specs=in_specs,
            out_specs=out_specs,
            check_vma=False,
        )(*args)

    return run
```

time: 40.9 us -> 30 us (0.73)
  Pallas kernels: 38.6 us -> 26.1 us
  local copies, waits for them, and re-layouts: 1.33 us -> 3.06 us
    pallas_call x3 -> x1, Pallas kernels: 38.6 us -> 26.1 us  [body(): pl.pallas_call(functools.partial(kernel, dims), out_shape=(jax.ShapeDtype...]
    unnamed x2, local copies, waits for them, and re-layouts: 0.65 us -> 3.06 us
    another operation x1 -> x0, local copies, waits for them, and re-layouts: 0.66 us -> none  [body(): return (remapped, sums[0, :3 * groups].reshape(3, groups))]
where the time goes in v1:
time: 30 us; the launch traced here: 29.8 us
  Pallas kernels  26.1 us (87%)
  local copies, waits for them, and re-layouts  3.06 us (10%)
  between operations  0.64 us (2%)
    pallas_call x1, Pallas kernels, body(): pl.pallas_call(functools.partial(kernel, dims), out_shape=(jax.ShapeDtype...  26.1 us
    unnamed x2, local copies, waits for them, and re-layouts  3.06 us

profile of v1, /device:TPU:0, one launch (start us, length us, event | category | flops | bytes accessed | tf_op | source)
XLA Modules:
  0.0 29.8 jit_solution(14361586037110583203)
XLA Ops:
  0.6 26.1 %ocean.1 = (bf16[3,8,4,1792]{3,2,1,0:T(4,128)(2,1)}, f32[3,8]{1,0:T(4,128)}) custom-call(f32[8,96,256]{2,1,0:T(8,128)} %temp_hbm.1, f32[8,96,256]{2,1,0:T(8,128)} %salt_hbm.1, bf16[8,96,256]{2,1,0:T(8,128)(2,1)} %zonal_hbm.1, bf16[8,96,256]{2,1,0:T(8,128)(2,1)} %merid_hbm.1, bf16[14,512,128]{2,1,0:T(8,128)(2,1)} %panel_hbm.1, f32[8]{0:T(128)} %kappa_ref.1, ...), custom_call_target="tpu_custom_call" | custom-call | tf_op jit(solution)/shard_map/ocean/pallas_call | solution.py:645
  26.7 1.8 %copy.15 = bf16[3,8,4,1792]{3,2,1,0:T(4,128)(2,1)} copy(bf16[3,8,4,1792]{3,2,1,0:T(4,128)(2,1)} %get-tuple-element.4) | data formatting | bytes 688128
  28.5 1.2 %copy.16 = f32[3,8]{1,0:T(4,128)} copy(f32[3,8]{1,0:T(4,128)} %get-tuple-element.5) | data formatting | bytes 192

commit v2 on v1

--- a/solution.py
+++ b/solution.py
@@ -50,14 +50,20 @@
     zonal_hbm,
     merid_hbm,
     panel_hbm,
+    kappa_hbm,
+    land_hbm,
+    start_hbm,
+    cluster_hbm,
+    area_hbm,
+    band_hbm,
+    out_ref,
+    sums_ref,
     kappa_ref,
     land_ref,
     start_ref,
     cluster_ref,
     area_ref,
     band_ref,
-    out_hbm,
-    sums_ref,
     x0,
     x1,
     uv,
@@ -74,9 +80,9 @@
     panel,
     shifted,
     result,
-    out_vmem,
     gather,
     in_sems,
+    small_sems,
     panel_sems,
     halo_send_sems,
     halo_recv_sems,
@@ -86,7 +92,6 @@
     e_send_sems,
     e_recv_sems,
     sum_sems,
-    out_sem,
 ):
     n_role, n_gy, n_gx, levels, cy, cx, trows, srows, nblk, sw, tb, groups = dims
     role, gy, gx = position()
@@ -99,6 +104,19 @@
     nk = EDGE * levels
     peer = functools.partial(peer_of, dims)
 
+    smalls = (
+        (kappa_hbm, kappa_ref),
+        (land_hbm, land_ref),
+        (band_hbm, band_ref),
+        (start_hbm, start_ref),
+        (cluster_hbm, cluster_ref),
+        (area_hbm, area_ref),
+    )
+    small_loads = [
+        pltpu.make_async_copy(src, dst, small_sems.at[i]) for i, (src, dst) in enumerate(smalls)
+    ]
+    for load in small_loads:
+        load.start()
     sources = ((temp_hbm, x0.at[0]), (salt_hbm, x0.at[1]), (zonal_hbm, uv.at[0]), (merid_hbm, uv.at[1]))
     loads = [pltpu.make_async_copy(src, dst, in_sems.at[i]) for i, (src, dst) in enumerate(sources)]
     for load in loads:
@@ -147,6 +165,8 @@
             flag = jnp.where(jnp.full((1, cx), land_ref[i], jnp.int32) == number, 0.0, flag)
         return flag
 
+    for load in small_loads:
+        load.wait()
     ocean = ocean_of(0, 0)
 
     band_rows[...] = jnp.zeros_like(band_rows)
@@ -595,9 +615,7 @@
         for f in range(3):
             for i in range(lev_grp):
                 row = h * half_rows + f * lev_rows + i * trows
-                out_vmem[f, h * lev_grp + i] = result[pl.ds(row, trows), :].astype(BF16)
-    store = pltpu.make_async_copy(out_vmem, out_hbm, out_sem)
-    store.start()
+                out_ref[f, h * lev_grp + i] = result[pl.ds(row, trows), :].astype(BF16)
 
     for can_send, _, copy in halos:
         when(can_send, copy.wait_send)
@@ -606,13 +624,23 @@
             bulk(h, d)[1].wait_send()
     for copy in e_copies:
         copy.wait_send()
-    store.wait()
     every = gather.at[pl.ds(0, total - 1)]
     for i in (1, 0):
         pltpu.make_async_copy(every, every, sum_sems.at[i]).wait()
     sums = jnp.sum(gather[...], axis=0)
     for f in range(3):
         sums_ref[pl.ds(f, 1), :] = turn(sums, -f * groups, 1)[:, :groups]
+
+
+def store_kernel(remapped_ref, sums_ref, remapped_hbm, sums_hbm, sems):
+    copies = [
+        pltpu.make_async_copy(remapped_ref, remapped_hbm, sems.at[0]),
+        pltpu.make_async_copy(sums_ref, sums_hbm, sems.at[1]),
+    ]
+    for copy in copies:
+        copy.start()
+    for copy in copies:
+        copy.wait()
 
 
 def body(
@@ -635,22 +663,27 @@
     halves = levels // lev_grp
     half_rows = 3 * lev_grp * trows
     glanes = -(-3 * groups // LANES) * LANES
-    hbm = pl.BlockSpec(memory_space=pl.ANY)
-    smem = pl.BlockSpec(memory_space=pltpu.SMEM)
+    hbm = pl.BlockSpec(memory_space=pltpu.MemorySpace.HBM)
     vmem = pl.BlockSpec(memory_space=pltpu.VMEM)
     brows = -(-n_gx * trows // LANES) * LANES
     dma = pltpu.SemaphoreType.DMA
     columns = n_gx * cx
     out_rows = halves * half_rows
-    return pl.pallas_call(
+    remapped, sums = pl.pallas_call(
         functools.partial(kernel, dims),
         out_shape=(
             jax.ShapeDtypeStruct((3, levels, trows, nblk * tb), BF16),
             jax.ShapeDtypeStruct((3, groups), F32),
         ),
-        in_specs=[hbm] * 5 + [smem] * 5 + [vmem],
-        out_specs=(hbm, vmem),
+        in_specs=[hbm] * 11,
+        out_specs=(vmem, vmem),
         scratch_shapes=[
+            pltpu.SMEM(mixing_coefficient.shape, F32),
+            pltpu.SMEM(continent_patch_numbering.shape, jnp.int32),
+            pltpu.SMEM(panel_starting_source_meridian.shape, jnp.int32),
+            pltpu.SMEM(target_parallel_cluster.shape, jnp.int32),
+            pltpu.SMEM(area.shape, F32),
+            pltpu.VMEM(parallel_band_coefficients.shape, BF16),
             pltpu.VMEM((2, levels, cy, cx), F32),
             pltpu.VMEM((2, levels, cy, cx), F32),
             pltpu.VMEM((2, levels, cy, cx), BF16),
@@ -667,9 +700,9 @@
             pltpu.VMEM((nblk, sw, tb), BF16),
             pltpu.VMEM((nblk, sw + LANES, tb), BF16),
             pltpu.VMEM((out_rows, nblk * tb), F32),
-            pltpu.VMEM((3, levels, trows, nblk * tb), BF16),
             pltpu.VMEM((total, 1, glanes), F32),
             dma((4,)),
+            dma((6,)),
             dma((nblk,)),
             dma((18,)),
             dma((18,)),
@@ -679,25 +712,41 @@
             dma((n_gx,)),
             dma((n_gx,)),
             dma((2,)),
-            dma(()),
         ],
         compiler_params=pltpu.CompilerParams(
-            collective_id=0, has_side_effects=True, vmem_limit_bytes=60 * 1024 * 1024
+            collective_id=0, has_side_effects=True, vmem_limit_bytes=26 * 1024 * 1024
         ),
         name="ocean",
     )(
-        thermal_anomaly,
-        saltiness_anomaly,
-        zonal_flow_fraction,
-        meridional_flow_fraction,
-        meridian_panel_coefficients,
-        mixing_coefficient,
-        continent_patch_numbering,
-        panel_starting_source_meridian,
-        target_parallel_cluster,
-        jnp.asarray(area),
-        parallel_band_coefficients,
+        *(
+            pltpu.with_memory_space_constraint(array, pltpu.MemorySpace.HBM)
+            for array in (
+                thermal_anomaly,
+                saltiness_anomaly,
+                zonal_flow_fraction,
+                meridional_flow_fraction,
+                meridian_panel_coefficients,
+                mixing_coefficient,
+                continent_patch_numbering,
+                panel_starting_source_meridian,
+                target_parallel_cluster,
+                jnp.asarray(area),
+                parallel_band_coefficients,
+            )
+        )
     )
+    return pl.pallas_call(
+        store_kernel,
+        out_shape=(
+            jax.ShapeDtypeStruct(remapped.shape, BF16),
+            jax.ShapeDtypeStruct(sums.shape, F32),
+        ),
+        in_specs=[vmem, vmem],
+        out_specs=(hbm, hbm),
+        scratch_shapes=[dma((2,))],
+        compiler_params=pltpu.CompilerParams(vmem_limit_bytes=4 * 1024 * 1024),
+        name="store",
+    )(remapped, sums)
 
 
 def solution(mesh):

time: 30 us -> 26.4 us (0.88)
  local copies, waits for them, and re-layouts: 3.06 us -> 0 us
  Pallas kernels: 26.1 us -> 25.6 us
    unnamed x2 -> x0, local copies, waits for them, and re-layouts: 3.06 us -> none
    pallas_call x1, Pallas kernels: 26.1 us -> 24.8 us  [body(): pl.pallas_call(functools.partial(kernel, dims), out_shape=(jax.ShapeDtype...]
    pallas_call x0 -> x1, Pallas kernels: none -> 0.75 us  [body(): pl.pallas_call(store_kernel, out_shape=(jax.ShapeDtypeStruct(remapped.sha...]
where the time goes in v2:
time: 26.4 us; the launch traced here: 26.2 us
  Pallas kernels  25.6 us (97%)
  between operations  0.64 us (2%)
    pallas_call x1, Pallas kernels, body(): pl.pallas_call(functools.partial(kernel, dims), out_shape=(jax.ShapeDtype...  24.8 us
    pallas_call x1, Pallas kernels, body(): pl.pallas_call(store_kernel, out_shape=(jax.ShapeDtypeStruct(remapped.sha...  0.75 us

profile of v2, /device:TPU:0, one launch (start us, length us, event | category | flops | bytes accessed | tf_op | source)
XLA Modules:
  0.0 26.2 jit_solution(15755646769190725724)
XLA Ops:
  0.6 24.8 %ocean.1 = (bf16[3,8,4,1792]{3,2,1,0:T(4,128)(2,1)S(1)}, f32[3,8]{1,0:T(4,128)S(1)}) custom-call(f32[8,96,256]{2,1,0:T(8,128)} %temp_hbm.1, f32[8,96,256]{2,1,0:T(8,128)} %salt_hbm.1, bf16[8,96,256]{2,1,0:T(8,128)(2,1)} %zonal_hbm.1, bf16[8,96,256]{2,1,0:T(8,128)(2,1)} %merid_hbm.1, bf16[14,512,128]{2,1,0:T(8,128)(2,1)} %panel_hbm.1, f32[8]{0:T(128)} %kappa_hbm.1, ...), custom_call_target="tpu_custom_call" | custom-call | tf_op jit(solution)/shard_map/ocean/pallas_call | solution.py:672
  25.5 0.8 %store.1 = (bf16[3,8,4,1792]{3,2,1,0:T(4,128)(2,1)}, f32[3,8]{1,0:T(4,128)}) custom-call(bf16[3,8,4,1792]{3,2,1,0:T(4,128)(2,1)S(1)} %get-tuple-element.4.remapped_ref, f32[3,8]{1,0:T(4,128)S(1)} %get-tuple-element.5.sums_ref), custom_call_target="tpu_custom_call" | custom-call | tf_op jit(solution)/shard_map/store/pallas_call | solution.py:738

commit v3 on v2

--- a/solution.py
+++ b/solution.py
@@ -12,6 +12,7 @@
 LANES = 128
 SUB = 8
 EDGE = 4
+SPLIT = 3
 F32 = jnp.float32
 BF16 = jnp.bfloat16
 MESH = pl.DeviceIdType.MESH
@@ -29,6 +30,17 @@
     size = value.shape[axis]
     shift = shift % size
     return pltpu.roll(value, shift, axis) if shift else value
+
+
+def partner(index, d, count):
+    if count & (count - 1):
+        return wrap(index + d, count)
+    other = index
+    for bit in range(count.bit_length() - 1):
+        if d >> bit & 1:
+            step = 1 << bit
+            other = other + step - 2 * step * lax.rem(lax.div(index, step), 2)
+    return other
 
 
 def position():
@@ -71,6 +83,9 @@
     halo_x,
     halo_uv,
     cols,
+    fold_send,
+    fold_recv,
+    chosen,
     band_rows,
     lat_send,
     lat,
@@ -118,14 +133,20 @@
     for load in small_loads:
         load.start()
     sources = ((temp_hbm, x0.at[0]), (salt_hbm, x0.at[1]), (zonal_hbm, uv.at[0]), (merid_hbm, uv.at[1]))
-    loads = [pltpu.make_async_copy(src, dst, in_sems.at[i]) for i, (src, dst) in enumerate(sources)]
-    for load in loads:
-        load.start()
+    loads = []
+    for h in range(halves):
+        part = pl.ds(h * lev_grp, lev_grp)
+        loads.append(
+            [
+                pltpu.make_async_copy(src.at[part], dst.at[part], in_sems.at[h, i])
+                for i, (src, dst) in enumerate(sources)
+            ]
+        )
+        for load in loads[h]:
+            load.start()
     panel_loads = [
         pltpu.make_async_copy(panel_hbm.at[j], panel.at[j], panel_sems.at[j]) for j in range(nblk)
     ]
-    for load in panel_loads:
-        load.start()
 
     barrier = pltpu.get_barrier_semaphore()
     greeted = set(range(1, n_gx)) | {d * n_gx for d in range(1, n_role * n_gy)}
@@ -136,6 +157,9 @@
     for d in greeted:
         pl.semaphore_signal(barrier, inc=1, device_id=peer(d), device_id_type=MESH)
 
+    lane = iota((1, LANES), 1)
+    quad = lax.div(lane, EDGE)
+    col = lax.rem(lane, EDGE)
     has_below = gy > 0
     has_above = gy < n_gy - 1
 
@@ -154,7 +178,8 @@
             cols[i, pl.ds(SUB + cy, SUB)] = jnp.zeros((SUB, LANES), F32)
 
     columns = n_gx * cx
-    lat[columns // LANES] = jnp.zeros((halves * half_rows, LANES), BF16)
+    for h in range(halves):
+        lat[h][columns // LANES] = jnp.zeros((half_rows, LANES), BF16)
 
     def ocean_of(dy, dx):
         ty = gy + dy
@@ -169,6 +194,12 @@
         load.wait()
     ocean = ocean_of(0, 0)
 
+    chosen[...] = jnp.zeros_like(chosen)
+    for q in range(2 * levels):
+        for side, (base, top) in enumerate(((0, 0), (LANES - 16, LANES - EDGE))):
+            ck, cl = iota((16, LANES), 0) + base, iota((16, LANES), 1)
+            hit = (ck >= top) & (ck < top + EDGE) & (ck - top == cl - 2 * nk - EDGE * q)
+            chosen[side, pl.ds(q * LANES + base, 16)] = jnp.where(hit, 1.0, 0.0).astype(BF16)
     band_rows[...] = jnp.zeros_like(band_rows)
     for g in range(n_gx):
         band_rows[pl.ds(g * trows, trows), pl.ds(0, srows)] = band_ref[g].astype(F32)
@@ -189,30 +220,138 @@
     )
     band = jnp.where(keep, spread, 0.0).astype(BF16)
 
-    lane = iota((1, LANES), 1)
-    quad = lax.div(lane, EDGE)
-    col = lax.rem(lane, EDGE)
-
-    for load in loads:
+    level0 = role * levels
+
+    def stencil(u, v, kap):
+        return 1.0 - 4.0 * kap, kap - u, kap + u, kap - v, kap + v
+
+    def advance(c, e, w, n, b, coef):
+        own, to_e, to_w, to_n, to_b = coef
+        return (own * c + (to_e * e + to_w * w)) + (to_n * n + to_b * b)
+
+    def whole(c, coef):
+        tiles_of = range(len(c))
+        left = [turn(a, -1, 1) for a in c]
+        right = [turn(a, 1, 1) for a in c]
+        out = []
+        for i in tiles_of:
+            e = jnp.where(lane == LANES - 1, left[i + 1], left[i]) if i + 1 < len(c) else left[i]
+            w = jnp.where(lane == 0, right[i - 1], right[i]) if i else right[i]
+            out.append(advance(c[i], e, w, turn(c[i], -1, 0), turn(c[i], 1, 0), coef[i]))
+        return out
+
+    def mean_fields(t1, s1, t2, s2, factor):
+        t, s = t1 + t2, s1 + s2
+        rho = 0.39 * s - (0.5 * factor) * t - 0.01 * (t1 * t1 + t2 * t2)
+        return 0.5 * t, 0.5 * s, rho
+
+    def factor_of(l):
+        return 0.17 * (1.0 + 0.03 * (level0 + l).astype(F32))
+
+    flag0 = ocean[:, :LANES]
+    half0 = 0.5 * flag0
+    wide = iota((1, cx), 1)
+    at_edge = (wide < 2) | (wide >= cx - 2)
+    tiles = cx // LANES
+    order = list(range(n_gx - 1, 0, -1))
+    at_end = (gx == 0) | (gx == n_gx - 1)
+
+    def bulk(h, d):
+        target = partner(gx, d, n_gx)
+        return target, pltpu.make_async_remote_copy(
+            src_ref=lat_send.at[h, target],
+            dst_ref=lat[h].at[pl.ds(gx * tiles, tiles)],
+            send_sem=a2a_send_sems.at[h, d],
+            recv_sem=a2a_recv_sems.at[h, d],
+            device_id=(role, gy, target),
+            device_id_type=MESH,
+        )
+
+    def local(h):
+        return pltpu.make_async_copy(
+            lat_send.at[h, gx],
+            lat[h].at[pl.ds(gx * tiles, tiles)],
+            local_sems.at[h],
+        )
+
+    def stage(h, g, f, rows):
+        for i in range(tiles):
+            lat_send[h, g, i, pl.ds(f * lev_rows, lev_rows)] = rows[
+                :, i * LANES : (i + 1) * LANES
+            ]
+
+    def main_levels(first_level, last_level):
+        for l in range(first_level, last_level):
+            kap = kappa_ref[l] * flag0
+            spans = [pl.ds(i * LANES, LANES) for i in range(tiles)]
+            coef = [
+                stencil(
+                    uv[0, l, :, span].astype(F32) * half0, uv[1, l, :, span].astype(F32) * half0, kap
+                )
+                for span in spans
+            ]
+            one = [whole([x0[t, l, :, span] for span in spans], coef) for t in range(2)]
+            two = [whole(one[t], coef) for t in range(2)]
+            factor = factor_of(l)
+            for i, span in enumerate(spans):
+                x1[0, l, :, span] = one[0][i]
+                x1[1, l, :, span] = one[1][i]
+                fields = mean_fields(one[0][i], one[1][i], two[0][i], two[1][i], factor)
+                for f in range(3):
+                    means[f, l, :, span] = fields[f].astype(BF16)
+
+    def main_lat(h):
+        for f in range(3):
+            rows = means[f, pl.ds(h * lev_grp, lev_grp)].reshape(in_r, cx)
+            got = jnp.dot(band[lev_rows : out_r - lev_rows], rows, preferred_element_type=F32)
+            got = jnp.where(at_edge, 0.0, got).astype(BF16)
+            for g in range(1, n_gx - 1):
+                stage(h, g, f, got[(g - 1) * lev_rows : g * lev_rows])
+
+    def held(target):
+        return (target == n_gx // 2 - 1) | (target == n_gx // 2)
+
+    def send_half(h):
+        for d in order:
+            target, copy = bulk(h, d)
+            now = (target > 0) & (target < n_gx - 1)
+            if h == halves - 1:
+                now = now & jnp.logical_not(held(target))
+            pl.when(now)(copy.start)
+        pl.when(jnp.logical_not(at_end))(local(h).start)
+
+    for load in loads[0]:
         load.wait()
-    first = jnp.zeros((cy, LANES), F32)
-    last = jnp.zeros((cy, LANES), F32)
-    for q in range(4 * levels):
-        kind, l = q // levels, q % levels
-        source = x0.at[kind, l] if kind < 2 else uv.at[kind - 2, l]
-        head = source[:, pl.ds(0, LANES)].astype(F32)
-        tail = source[:, pl.ds(cx - LANES, LANES)].astype(F32)
-        first = jnp.where(quad == q, turn(head, EDGE * q, 1), first)
-        last = jnp.where(quad == q, turn(tail, EDGE * (q + 1), 1), last)
+    main_levels(0, SPLIT)
+    for later in loads[1:]:
+        for load in later:
+            load.wait()
+    packed = []
+    for side, edge in enumerate((pl.ds(0, LANES), pl.ds(cx - LANES, LANES))):
+        block = jnp.concatenate(
+            [uv[q // levels, q % levels, :, edge] for q in range(2 * levels)], axis=1
+        )
+        block = jnp.dot(block, chosen[side], preferred_element_type=F32)
+        for q in range(2 * levels):
+            tile = x0[q // levels, q % levels, :, edge]
+            block = jnp.where(quad == q, turn(tile, EDGE * (q + side), 1), block)
+        packed.append(block)
+    first, last = packed
     cols[1, pl.ds(SUB, cy)] = first
     cols[2, pl.ds(SUB, cy)] = last
+    mid = cy // 2
+
+    def fold(block):
+        return jnp.where(lane < 2 * nk, block[:mid], turn(block[mid:], 2 * nk, 1))
+
+    fold_send[0] = fold(jnp.where(col < 2, first, turn(first, 2 - 2 * nk, 1)))
+    fold_send[1] = fold(jnp.where(col < 2, turn(last, -2 - 2 * nk, 1), last))
 
     west = wrap(gx + n_gx - 1, n_gx)
     east = wrap(gx + 1, n_gx)
-    own_w, own_e = cols.at[1, pl.ds(SUB, cy)], cols.at[2, pl.ds(SUB, cy)]
     plan = [
-        (None, None, own_w, cols.at[3, pl.ds(SUB, cy)], (role, gy, west)),
-        (None, None, own_e, cols.at[0, pl.ds(SUB, cy)], (role, gy, east)),
+        (None, None, fold_send.at[0], fold_recv.at[0], (role, gy, west)),
+        (None, None, fold_send.at[1], fold_recv.at[1], (role, gy, east)),
     ]
     for side, (can_send, can_recv) in enumerate(((has_below, has_above), (has_above, has_below))):
         ty = gy - 1 if side == 0 else gy + 1
@@ -275,83 +414,24 @@
     pl.semaphore_wait(barrier, len(greeted))
     for can_send, _, copy in halos:
         when(can_send, copy.start)
-
-    level0 = role * levels
-
-    def advance(c, e, w, n, b, u, v, kap):
-        return (1.0 - 4.0 * kap) * c + (kap * (e + w + n + b) - u * (e - w) - v * (n - b))
-
-    def whole(c, u, v, kap):
-        return advance(
-            c, turn(c, -1, 1), turn(c, 1, 1), turn(c, -1, 0), turn(c, 1, 0), u, v, kap
-        )
-
-    def density(temp, salt, factor):
-        return 0.78 * salt - factor * temp - 0.02 * temp * temp
-
-    def factor_of(l):
-        return 0.17 * (1.0 + 0.03 * (level0 + l).astype(F32))
-
-    wide = iota((1, cx), 1)
-    at_edge = (wide < 2) | (wide >= cx - 2)
-    tiles = cx // LANES
-    order = sorted(range(1, n_gx), key=lambda d: -min(d, n_gx - d))
-    at_end = (gx == 0) | (gx == n_gx - 1)
-
-    def bulk(h, d):
-        target = wrap(gx + d, n_gx)
-        return target, pltpu.make_async_remote_copy(
-            src_ref=lat_send.at[h, target],
-            dst_ref=lat.at[pl.ds(gx * tiles, tiles), pl.ds(h * half_rows, half_rows)],
-            send_sem=a2a_send_sems.at[h, d],
-            recv_sem=a2a_recv_sems.at[h, d],
-            device_id=(role, gy, target),
-            device_id_type=MESH,
-        )
-
-    def local(h):
-        return pltpu.make_async_copy(
-            lat_send.at[h, gx],
-            lat.at[pl.ds(gx * tiles, tiles), pl.ds(h * half_rows, half_rows)],
-            local_sems.at[h],
-        )
-
-    def stage(h, g, f, rows):
-        for i in range(tiles):
-            lat_send[h, g, i, pl.ds(f * lev_rows, lev_rows)] = rows[
-                :, i * LANES : (i + 1) * LANES
-            ]
-
-    for h in range(halves):
-        for l in range(h * lev_grp, (h + 1) * lev_grp):
-            u = uv[0, l].astype(F32) * (0.5 * ocean)
-            v = uv[1, l].astype(F32) * (0.5 * ocean)
-            kap = kappa_ref[l] * ocean
-            one = [whole(x0[t, l], u, v, kap) for t in range(2)]
-            two = [whole(one[t], u, v, kap) for t in range(2)]
-            factor = factor_of(l)
-            r1 = density(one[0], one[1], factor)
-            r2 = density(two[0], two[1], factor)
-            x1[0, l] = one[0]
-            x1[1, l] = one[1]
-            means[0, l] = (0.5 * (one[0] + two[0])).astype(BF16)
-            means[1, l] = (0.5 * (one[1] + two[1])).astype(BF16)
-            means[2, l] = (0.5 * (r1 + r2)).astype(BF16)
-        for f in range(3):
-            rows = means[f, pl.ds(h * lev_grp, lev_grp)].reshape(in_r, cx)
-            got = jnp.dot(
-                band[lev_rows : out_r - lev_rows], rows, preferred_element_type=F32
-            )
-            got = jnp.where(at_edge, 0.0, got).astype(BF16)
-            for g in range(1, n_gx - 1):
-                stage(h, g, f, got[(g - 1) * lev_rows : g * lev_rows])
-        for d in order:
-            target, copy = bulk(h, d)
-            pl.when((target > 0) & (target < n_gx - 1))(copy.start)
-        pl.when(jnp.logical_not(at_end))(local(h).start)
+    main_levels(SPLIT, lev_grp)
+    main_lat(0)
+    send_half(0)
+    for load in panel_loads:
+        load.start()
+    for h in range(1, halves):
+        main_levels(h * lev_grp, (h + 1) * lev_grp)
+        main_lat(h)
+        send_half(h)
 
     for _, can_recv, copy in column_halos:
         when(can_recv, copy.wait_recv)
+    for i, (block, shift) in enumerate(((3, 2 * nk - 2), (0, 2 * nk + 2))):
+        got = fold_recv[i]
+        for part, tail in enumerate((got, turn(got, 2 * nk, 1))):
+            cols[block, pl.ds(SUB + part * mid, mid)] = jnp.where(
+                lane < 2 * nk, tail, turn(tail, shift, 1)
+            )
     cye = cy + 2 * SUB
     row_e = iota((cye, 1), 0)
     kap_l = jnp.zeros((1, LANES), F32)
@@ -371,17 +451,15 @@
         half = 0.5 * oc
         u = jnp.where(lane < nk, turn(block, -2 * nk, 1), turn(block, -nk, 1)) * half
         v = jnp.where(lane < nk, turn(block, -3 * nk, 1), turn(block, -2 * nk, 1)) * half
-        return u, v, kap_l * oc
+        return stencil(u, v, kap_l * oc)
 
     def step_left(left, right, coef):
         e = jnp.where(col == EDGE - 1, turn(right, EDGE - 1, 1), turn(left, -1, 1))
-        return advance(left, e, turn(left, 1, 1), turn(left, -1, 0), turn(left, 1, 0), *coef)
+        return advance(left, e, turn(left, 1, 1), turn(left, -1, 0), turn(left, 1, 0), coef)
 
     def step_right(left, right, coef):
         w = jnp.where(col == 0, turn(left, 1 - EDGE, 1), turn(right, 1, 1))
-        return advance(
-            right, turn(right, -1, 1), w, turn(right, -1, 0), turn(right, 1, 0), *coef
-        )
+        return advance(right, turn(right, -1, 1), w, turn(right, -1, 0), turn(right, 1, 0), coef)
 
     own = coefficients(1, 0)
     left1 = step_left(cols[0], cols[1], coefficients(0, -1))
@@ -393,14 +471,11 @@
     east2 = step_left(east1, right1, own)
     both1 = jnp.where(col < 2, west1, east1)[SUB : SUB + cy]
     both2 = jnp.where(col < 2, west2, east2)[SUB : SUB + cy]
-    rho = 0.5 * (
-        density(both1, turn(both1, -nk, 1), factor_l)
-        + density(both2, turn(both2, -nk, 1), factor_l)
+    temp_salt, _, rho = mean_fields(
+        both1, turn(both1, -nk, 1), both2, turn(both2, -nk, 1), factor_l
     )
     packed = jnp.where(
-        lane < 2 * nk,
-        0.5 * (both1 + both2),
-        jnp.where(lane < 3 * nk, turn(rho, 2 * nk, 1), 0.0),
+        lane < 2 * nk, temp_salt, jnp.where(lane < 3 * nk, turn(rho, 2 * nk, 1), 0.0)
     ).astype(BF16)
     narrow = n_gx * trows
     thin = jnp.dot(flat[:narrow], pick_c[:, :cy], preferred_element_type=F32)
@@ -412,7 +487,7 @@
 
     e_copies = []
     for d in order:
-        target = wrap(gx + d, n_gx)
+        target = partner(gx, d, n_gx)
         copy = pltpu.make_async_remote_copy(
             src_ref=e_send.at[target],
             dst_ref=e_recv.at[gx],
@@ -436,43 +511,43 @@
     def down(a, b):
         return jnp.where(sub8 == 0, turn(a, 1, 0), turn(b, 1, 0))
 
-    def rows_step(c, n, b, u, v, kap):
-        return advance(c, turn(c, -1, 1), turn(c, 1, 1), n, b, u, v, kap)
+    def rows_step(c, n, b, coef):
+        return advance(c, turn(c, -1, 1), turn(c, 1, 1), n, b, coef)
 
     for l in range(levels):
         kap = kappa_ref[l] * ocean
         factor = factor_of(l)
         flow = [uv[i, l, pl.ds(0, 16)].astype(F32)[:SUB] * (0.5 * ocean) for i in range(2)]
         other = [halo_uv[0, i, l].astype(F32) * (0.5 * ocean_below) for i in range(2)]
-        kap_o = kappa_ref[l] * ocean_below
+        flow = stencil(*flow, kap)
+        other = stencil(*other, kappa_ref[l] * ocean_below)
         ones, twos = [], []
         for t in range(2):
             far, edge, near = halo_x[0, t, l], x0[t, l, pl.ds(0, SUB)], x0[t, l, pl.ds(SUB, SUB)]
-            out1 = rows_step(far, up(far, edge), turn(far, 1, 0), *other, kap_o)
-            in1 = rows_step(edge, up(edge, near), down(far, edge), *flow, kap)
+            out1 = rows_step(far, up(far, edge), turn(far, 1, 0), other)
+            in1 = rows_step(edge, up(edge, near), down(far, edge), flow)
             ones.append(in1)
             next1 = x1[t, l, pl.ds(SUB, SUB)]
-            twos.append(rows_step(in1, up(in1, next1), down(out1, in1), *flow, kap))
-        r = density(*ones, factor) + density(*twos, factor)
-        for f, value in enumerate((ones[0] + twos[0], ones[1] + twos[1], r)):
-            means[f, l, pl.ds(0, SUB)] = (0.5 * value).astype(BF16)
+            twos.append(rows_step(in1, up(in1, next1), down(out1, in1), flow))
+        for f, value in enumerate(mean_fields(*ones, *twos, factor)):
+            means[f, l, pl.ds(0, SUB)] = value.astype(BF16)
 
         flow = [uv[i, l, pl.ds(cy - 16, 16)].astype(F32)[SUB:] * (0.5 * ocean) for i in range(2)]
         other = [halo_uv[1, i, l].astype(F32) * (0.5 * ocean_above) for i in range(2)]
-        kap_o = kappa_ref[l] * ocean_above
+        flow = stencil(*flow, kap)
+        other = stencil(*other, kappa_ref[l] * ocean_above)
         ones, twos = [], []
         for t in range(2):
             far = halo_x[1, t, l]
             edge = x0[t, l, pl.ds(cy - SUB, SUB)]
             near = x0[t, l, pl.ds(cy - 2 * SUB, SUB)]
-            out1 = rows_step(far, turn(far, -1, 0), down(edge, far), *other, kap_o)
-            in1 = rows_step(edge, up(edge, far), down(near, edge), *flow, kap)
+            out1 = rows_step(far, turn(far, -1, 0), down(edge, far), other)
+            in1 = rows_step(edge, up(edge, far), down(near, edge), flow)
             ones.append(in1)
             next1 = x1[t, l, pl.ds(cy - 2 * SUB, SUB)]
-            twos.append(rows_step(in1, up(in1, out1), down(next1, in1), *flow, kap))
-        r = density(*ones, factor) + density(*twos, factor)
-        for f, value in enumerate((ones[0] + twos[0], ones[1] + twos[1], r)):
-            means[f, l, pl.ds(cy - SUB, SUB)] = (0.5 * value).astype(BF16)
+            twos.append(rows_step(in1, up(in1, out1), down(next1, in1), flow))
+        for f, value in enumerate(mean_fields(*ones, *twos, factor)):
+            means[f, l, pl.ds(cy - SUB, SUB)] = value.astype(BF16)
 
     ends = jnp.concatenate([band[:lev_rows], band[out_r - lev_rows :]], axis=0)
     for h in range(halves):
@@ -486,6 +561,10 @@
             target, copy = bulk(h, d)
             pl.when((target == 0) | (target == n_gx - 1))(copy.start)
         pl.when(at_end)(local(h).start)
+
+    for d in order:
+        target, copy = bulk(halves - 1, d)
+        pl.when(held(target))(copy.start)
 
     depth = sw + LANES
     sub = iota((1, SUB, 1), 1)
@@ -572,20 +651,23 @@
         for i in range(tiles):
             placed[s * tiles + i] = put[:, i * LANES : (i + 1) * LANES]
 
+    weighted = []
     for h in range(halves):
         for d in order:
             bulk(h, d)[1].wait_recv()
         local(h).wait()
-    for i in range(n_gx * tiles):
-        lat[i] = lat[i] + placed[i]
-    squares = jnp.zeros((out_rows, tb), F32)
-    for j in range(nblk):
-        tile = tile_of(j)
-        window = jnp.concatenate([lat[tile + i] for i in range(depth // LANES)], axis=1)
-        values = jnp.dot(window, shifted[j], preferred_element_type=F32)
-        squares = squares + values * values
-        result[:, pl.ds(j * tb, tb)] = values
-    weighted = jnp.sum(squares, axis=1, keepdims=True) * hot
+        rows = pl.ds(h * half_rows, half_rows)
+        for i in range(n_gx * tiles):
+            lat[h][i] = lat[h][i] + placed[i, rows]
+        squares = jnp.zeros((half_rows, tb), F32)
+        for j in range(nblk):
+            tile = tile_of(j)
+            window = jnp.concatenate([lat[h][tile + i] for i in range(depth // LANES)], axis=1)
+            values = jnp.dot(window, shifted[j], preferred_element_type=F32)
+            squares = squares + values * values
+            result[rows, pl.ds(j * tb, tb)] = values
+        weighted.append(jnp.sum(squares, axis=1, keepdims=True))
+    weighted = jnp.concatenate(weighted, axis=0) * hot
     part = jnp.sum(weighted, axis=0, keepdims=True) / denom
 
     def for_others(do):
@@ -691,9 +773,14 @@
             pltpu.VMEM((2, 2, levels, SUB, cx), F32),
             pltpu.VMEM((2, 2, levels, SUB, cx), BF16),
             pltpu.VMEM((4, cy + 2 * SUB, LANES), F32),
+            pltpu.VMEM((2, cy // 2, LANES), F32),
+            pltpu.VMEM((2, cy // 2, LANES), F32),
+            pltpu.VMEM((2, 2 * levels * LANES, LANES), BF16),
             pltpu.VMEM((brows, LANES), F32),
             pltpu.VMEM((halves, n_gx, cx // LANES, half_rows, LANES), BF16),
-            pltpu.VMEM((columns // LANES + 1, out_rows, LANES), BF16),
+            tuple(
+                pltpu.VMEM((columns // LANES + 1, half_rows, LANES), BF16) for _ in range(halves)
+            ),
             pltpu.VMEM((n_gx, trows, LANES), BF16),
             pltpu.VMEM((n_gx, trows, LANES), BF16),
             pltpu.VMEM((columns // LANES, out_rows, LANES), BF16),
@@ -701,7 +788,7 @@
             pltpu.VMEM((nblk, sw + LANES, tb), BF16),
             pltpu.VMEM((out_rows, nblk * tb), F32),
             pltpu.VMEM((total, 1, glanes), F32),
-            dma((4,)),
+            dma((halves, 4)),
             dma((6,)),
             dma((nblk,)),
             dma((18,)),

time: 26.4 us -> 25.4 us (0.962)
  Pallas kernels: 25.6 us -> 24.6 us
    pallas_call x1, Pallas kernels: 24.8 us -> 23.8 us  [body(): pl.pallas_call(functools.partial(kernel, dims), out_shape=(jax.ShapeDtype...]
where the time goes in v3:
time: 25.4 us; the launch traced here: 25.2 us
  Pallas kernels  24.6 us (97%)
  between operations  0.64 us (3%)
    pallas_call x1, Pallas kernels, body(): pl.pallas_call(functools.partial(kernel, dims), out_shape=(jax.ShapeDtype...  23.8 us
    pallas_call x1, Pallas kernels, body(): pl.pallas_call(store_kernel, out_shape=(jax.ShapeDtypeStruct(remapped.sha...  0.75 us

profile of v3, /device:TPU:0, one launch (start us, length us, event | category | flops | bytes accessed | tf_op | source)
XLA Modules:
  0.0 25.2 jit_solution(5101506561474189610)
XLA Ops:
  0.6 23.8 %ocean.1 = (bf16[3,8,4,1792]{3,2,1,0:T(4,128)(2,1)S(1)}, f32[3,8]{1,0:T(4,128)S(1)}) custom-call(f32[8,96,256]{2,1,0:T(8,128)} %temp_hbm.1, f32[8,96,256]{2,1,0:T(8,128)} %salt_hbm.1, bf16[8,96,256]{2,1,0:T(8,128)(2,1)} %zonal_hbm.1, bf16[8,96,256]{2,1,0:T(8,128)(2,1)} %merid_hbm.1, bf16[14,512,128]{2,1,0:T(8,128)(2,1)} %panel_hbm.1, f32[8]{0:T(128)} %kappa_hbm.1, ...), custom_call_target="tpu_custom_call" | custom-call | tf_op jit(solution)/shard_map/ocean/pallas_call | solution.py:754
  24.5 0.8 %store.1 = (bf16[3,8,4,1792]{3,2,1,0:T(4,128)(2,1)}, f32[3,8]{1,0:T(4,128)}) custom-call(bf16[3,8,4,1792]{3,2,1,0:T(4,128)(2,1)S(1)} %get-tuple-element.4.remapped_ref, f32[3,8]{1,0:T(4,128)S(1)} %get-tuple-element.5.sums_ref), custom_call_target="tpu_custom_call" | custom-call | tf_op jit(solution)/shard_map/store/pallas_call | solution.py:825

commit v4 on v3

--- a/solution.py
+++ b/solution.py
@@ -557,10 +557,11 @@
             got = jnp.where(at_edge, 0.0, got).astype(BF16)
             stage(h, 0, f, got[:lev_rows])
             stage(h, n_gx - 1, f, got[lev_rows:])
-        for d in order:
+        pl.when(at_end)(local(h).start)
+    for d in order:
+        for h in range(halves):
             target, copy = bulk(h, d)
             pl.when((target == 0) | (target == n_gx - 1))(copy.start)
-        pl.when(at_end)(local(h).start)
 
     for d in order:
         target, copy = bulk(halves - 1, d)

time: 25.4 us -> 25.2 us (level)
  no operation moved by 1% of the time
where the time goes in v4:
time: 25.2 us; the launch traced here: 25.1 us
  Pallas kernels  24.4 us (97%)
  between operations  0.64 us (3%)
    pallas_call x1, Pallas kernels, body(): pl.pallas_call(functools.partial(kernel, dims), out_shape=(jax.ShapeDtype...  23.7 us
    pallas_call x1, Pallas kernels, body(): pl.pallas_call(store_kernel, out_shape=(jax.ShapeDtypeStruct(remapped.sha...  0.75 us

profile of v4, /device:TPU:0, one launch (start us, length us, event | category | flops | bytes accessed | tf_op | source)
XLA Modules:
  0.0 25.1 jit_solution(4857852860578882385)
XLA Ops:
  0.6 23.7 %ocean.1 = (bf16[3,8,4,1792]{3,2,1,0:T(4,128)(2,1)S(1)}, f32[3,8]{1,0:T(4,128)S(1)}) custom-call(f32[8,96,256]{2,1,0:T(8,128)} %temp_hbm.1, f32[8,96,256]{2,1,0:T(8,128)} %salt_hbm.1, bf16[8,96,256]{2,1,0:T(8,128)(2,1)} %zonal_hbm.1, bf16[8,96,256]{2,1,0:T(8,128)(2,1)} %merid_hbm.1, bf16[14,512,128]{2,1,0:T(8,128)(2,1)} %panel_hbm.1, f32[8]{0:T(128)} %kappa_hbm.1, ...), custom_call_target="tpu_custom_call" | custom-call | tf_op jit(solution)/shard_map/ocean/pallas_call | solution.py:755
  24.3 0.8 %store.1 = (bf16[3,8,4,1792]{3,2,1,0:T(4,128)(2,1)}, f32[3,8]{1,0:T(4,128)}) custom-call(bf16[3,8,4,1792]{3,2,1,0:T(4,128)(2,1)S(1)} %get-tuple-element.4.remapped_ref, f32[3,8]{1,0:T(4,128)S(1)} %get-tuple-element.5.sums_ref), custom_call_target="tpu_custom_call" | custom-call | tf_op jit(solution)/shard_map/store/pallas_call | solution.py:826

commit v5 on v4

--- a/solution.py
+++ b/solution.py
@@ -424,14 +424,6 @@
         main_lat(h)
         send_half(h)
 
-    for _, can_recv, copy in column_halos:
-        when(can_recv, copy.wait_recv)
-    for i, (block, shift) in enumerate(((3, 2 * nk - 2), (0, 2 * nk + 2))):
-        got = fold_recv[i]
-        for part, tail in enumerate((got, turn(got, 2 * nk, 1))):
-            cols[block, pl.ds(SUB + part * mid, mid)] = jnp.where(
-                lane < 2 * nk, tail, turn(tail, shift, 1)
-            )
     cye = cy + 2 * SUB
     row_e = iota((cye, 1), 0)
     kap_l = jnp.zeros((1, LANES), F32)
@@ -461,6 +453,14 @@
         w = jnp.where(col == 0, turn(left, 1 - EDGE, 1), turn(right, 1, 1))
         return advance(right, turn(right, -1, 1), w, turn(right, -1, 0), turn(right, 1, 0), coef)
 
+    for _, can_recv, copy in column_halos:
+        when(can_recv, copy.wait_recv)
+    for i, (block, shift) in enumerate(((3, 2 * nk - 2), (0, 2 * nk + 2))):
+        got = fold_recv[i]
+        for part, tail in enumerate((got, turn(got, 2 * nk, 1))):
+            cols[block, pl.ds(SUB + part * mid, mid)] = jnp.where(
+                lane < 2 * nk, tail, turn(tail, shift, 1)
+            )
     own = coefficients(1, 0)
     left1 = step_left(cols[0], cols[1], coefficients(0, -1))
     west1 = step_right(cols[0], cols[1], own)

time: 25.2 us -> 25.2 us (level)
  no operation moved by 1% of the time
where the time goes in v5:
time: 25.2 us; the launch traced here: 25 us
  Pallas kernels  24.4 us (97%)
  between operations  0.64 us (3%)
    pallas_call x1, Pallas kernels, body(): pl.pallas_call(functools.partial(kernel, dims), out_shape=(jax.ShapeDtype...  23.6 us
    pallas_call x1, Pallas kernels, body(): pl.pallas_call(store_kernel, out_shape=(jax.ShapeDtypeStruct(remapped.sha...  0.75 us

profile of v5, /device:TPU:0, one launch (start us, length us, event | category | flops | bytes accessed | tf_op | source)
XLA Modules:
  0.0 25.0 jit_solution(11014417122530504742)
XLA Ops:
  0.6 23.6 %ocean.1 = (bf16[3,8,4,1792]{3,2,1,0:T(4,128)(2,1)S(1)}, f32[3,8]{1,0:T(4,128)S(1)}) custom-call(f32[8,96,256]{2,1,0:T(8,128)} %temp_hbm.1, f32[8,96,256]{2,1,0:T(8,128)} %salt_hbm.1, bf16[8,96,256]{2,1,0:T(8,128)(2,1)} %zonal_hbm.1, bf16[8,96,256]{2,1,0:T(8,128)(2,1)} %merid_hbm.1, bf16[14,512,128]{2,1,0:T(8,128)(2,1)} %panel_hbm.1, f32[8]{0:T(128)} %kappa_hbm.1, ...), custom_call_target="tpu_custom_call" | custom-call | tf_op jit(solution)/shard_map/ocean/pallas_call | solution.py:755
  24.3 0.8 %store.1 = (bf16[3,8,4,1792]{3,2,1,0:T(4,128)(2,1)}, f32[3,8]{1,0:T(4,128)}) custom-call(bf16[3,8,4,1792]{3,2,1,0:T(4,128)(2,1)S(1)} %get-tuple-element.4.remapped_ref, f32[3,8]{1,0:T(4,128)S(1)} %get-tuple-element.5.sums_ref), custom_call_target="tpu_custom_call" | custom-call | tf_op jit(solution)/shard_map/store/pallas_call | solution.py:826
